TPU v7x, 128 devices: a whole 4x4x4 slice. The times are simulated.
128 devices in a mesh: fsdp: 64 (over x_lo, y, z, core), grp: 2 (over x_hi).
Axes of the slice: x: 4 (x_hi: 2, x_lo: 2; x = x_hi * 2 + x_lo), y: 4, z: 4, core: 2. Of those that a mesh axis runs over, the one named last changes fastest.
Arguments:
- hidden: bfloat16 [32768, 3072], P('fsdp', 'grp'), may hold values from -16 to 16
- queries: bfloat16 [32768, 1536], P('fsdp', 'grp'), may hold values from -6 to 6
- attn_keys: bfloat16 [32768, 1536], P('fsdp', 'grp'), may hold values from -6 to 6
- w_value: bfloat16 [1536, 3072], P('fsdp', 'grp'), may hold values from -1 to 1
- w_out: bfloat16 [1536, 3072], P('fsdp', 'grp'), may hold values from -1 to 1
- alpha: float32 [3072], P('grp'), may hold values from 0.05 to 0.5
- out_grad: bfloat16 [32768, 3072], P('fsdp', 'grp'), may hold values from -6 to 6
Outputs:
- new_hidden: bfloat16 [32768, 3072], P('fsdp', 'grp')
- grad_hidden: bfloat16 [32768, 3072], P('fsdp', 'grp')
- grad_queries: bfloat16 [32768, 1536], P('fsdp', 'grp')
- grad_keys: bfloat16 [32768, 1536], P('fsdp', 'grp')
- grad_w_value: float32 [1536, 3072], P('fsdp', 'grp')
- grad_w_out: float32 [1536, 3072], P('fsdp', 'grp')
All inputs are finite; a program needn't handle non-finite values.
Results may differ from a plain program's by a relative error of at most 0.012.
The roundings to bfloat16 on the way count: a program that leaves them out, or rounds other values in their place, can miss the bound.
Values may be sent and summed in bfloat16 or wider, within the bound.
A program may use at most 192 MiB of HBM per device.

v0:
```python
import jax
import jax.numpy as jnp
from jax import lax
from jax.sharding import Mesh
from jax.sharding import PartitionSpec as P

D = 3072
HS = 128
FSDP = ("fsdp_0", "fsdp_1", "fsdp_2", "fsdp_3")


EPS = 1e-06


def from_everyone(value, axis):
    count = lax.axis_size(axis)
    return lax.all_to_all(
        jnp.broadcast_to(value[None], (count, *value.shape)), axis, 0, 0, tiled=True
    )


def of_everyone(value, axis):
    everything = from_everyone(value, axis)
    return jnp.sum(everything, axis=0)


def packed_total(arrays, axis):
    ends = [0]
    for a in arrays:
        ends.append(ends[-1] + a.size)
    subtotal = of_everyone(jnp.concatenate([a.ravel() for a in arrays]), axis)
    return tuple((subtotal[b:e].reshape(a.shape) for a, b, e in zip(arrays, ends, ends[1:])))


def sent_together(arrays, axis, dim, along):
    ends, at = ([], 0)
    for a in arrays[:-1]:
        at += a.shape[along]
        ends.append(at)
    both = jnp.concatenate(arrays, axis=along)
    return tuple(jnp.split(lax.all_gather(both, axis, axis=dim, tiled=True), ends, axis=along))


def cut_along(value, dim, count):
    before, after = (value.shape[:dim], value.shape[dim + 1 :])
    return jnp.moveaxis(value.reshape(*before, count, -1, *after), dim, 0)


def summed_on_arrival(value, axis, dim):
    tiles = cut_along(value, dim, lax.axis_size(axis))
    arrived = lax.all_to_all(tiles, axis, split_axis=0, concat_axis=0, tiled=True)
    return arrived.sum(axis=0)


def laid_out(tiles, dim):
    tiles = jnp.moveaxis(tiles, 0, dim)
    dims = tiles.shape
    return tiles.reshape(*dims[:dim], dims[dim] * dims[dim + 1], *dims[dim + 2 :])


def collect(value, axis, dim):
    return laid_out(from_everyone(value, axis), dim)


def summed_rows(value, chips, core, dim):
    sizes = (lax.axis_size(chips), lax.axis_size(core))
    tiles = cut_along(value, dim, sizes[0] * sizes[1])
    inside = tiles.shape[1:]
    tiles = tiles.reshape(*sizes, *inside).swapaxes(0, 1).reshape(-1, *inside)
    tiles = lax.psum_scatter(tiles, core, scatter_dimension=0, tiled=True)
    return lax.psum_scatter(tiles, chips, scatter_dimension=0, tiled=True)[0]


def contract_last(left, right):
    return lax.dot_general(
        left, right, (((1,), (1,)), ((), ())), preferred_element_type=jnp.float32
    )


def contract_first(left, right):
    return lax.dot_general(
        left, right, (((0,), (0,)), ((), ())), preferred_element_type=jnp.float32
    )


def causal_probs(query_head, key_head):
    length = query_head.shape[0]
    score_scale = query_head.shape[1] ** (-0.5)
    scores = contract_last(query_head, key_head) * score_scale
    row_pos = lax.broadcasted_iota(jnp.int32, (length, length), 0)
    col_pos = lax.broadcasted_iota(jnp.int32, (length, length), 1)
    scores = jnp.where(row_pos >= col_pos, scores, -1e30)
    row_peak = jnp.max(scores, axis=1, keepdims=True)
    exp_terms = jnp.exp(scores - row_peak)
    return exp_terms / jnp.sum(exp_terms, axis=1, keepdims=True)


def head_forward(items):
    query_head, key_head, value_head = items
    attn_prob = causal_probs(query_head, key_head)
    return jnp.dot(
        attn_prob.astype(jnp.bfloat16), value_head, preferred_element_type=jnp.float32
    ).astype(jnp.bfloat16)


def head_backward(items):
    query_head, key_head, value_head, grad_head = items
    score_scale = query_head.shape[1] ** (-0.5)
    attn_prob = causal_probs(query_head, key_head)
    prob_half = attn_prob.astype(jnp.bfloat16)
    grad_prob = contract_last(grad_head, value_head)
    row_delta = jnp.sum(attn_prob * grad_prob, axis=1, keepdims=True)
    grad_score = (attn_prob * (grad_prob - row_delta)).astype(jnp.bfloat16)
    grad_query = (
        jnp.dot(grad_score, key_head, preferred_element_type=jnp.float32) * score_scale
    ).astype(jnp.bfloat16)
    grad_key = (contract_first(grad_score, query_head) * score_scale).astype(jnp.bfloat16)
    grad_value = contract_first(prob_half, grad_head).astype(jnp.bfloat16)
    return (grad_query, grad_key, grad_value)


def split_heads(block):
    return block.reshape(block.shape[0], -1, HS).transpose(1, 0, 2)


def join_heads(stacked):
    return stacked.transpose(1, 0, 2).reshape(stacked.shape[1], -1)


def shards(hidden, queries, attn_keys, w_value, w_out, alpha, out_grad):
    half_width = hidden.shape[1]
    value_rows = w_value.astype(jnp.float32)
    out_rows = w_out.astype(jnp.float32)
    row_sums = packed_total(
        (jnp.sum(value_rows * value_rows, axis=1), jnp.sum(out_rows * out_rows, axis=1)), "grp"
    )
    norm_v = jnp.sqrt(row_sums[0] + EPS)[:, None]
    norm_o = jnp.sqrt(row_sums[1] + EPS)[:, None]
    unit_v = value_rows / norm_v
    unit_o = out_rows / norm_o
    weight_v, weight_o = sent_together(
        (unit_v.astype(jnp.bfloat16), unit_o.astype(jnp.bfloat16)), FSDP, 0, 1
    )
    value_parts = contract_last(hidden, weight_v)
    values_mine = summed_on_arrival(value_parts, "grp", 1).astype(jnp.bfloat16)
    q_heads = split_heads(queries)
    k_heads = split_heads(attn_keys)
    v_heads = split_heads(values_mine)
    attn_mine = join_heads(lax.map(head_forward, (q_heads, k_heads, v_heads)))
    attn_all = collect(attn_mine, "grp", 1)
    proj = jnp.dot(attn_all, weight_o, preferred_element_type=jnp.float32)
    hidden_f = hidden.astype(jnp.float32)
    keep_rate = 1.0 - alpha
    moments = packed_total(
        (
            jnp.sum(proj * proj, axis=1),
            jnp.sum(keep_rate * keep_rate * hidden_f * hidden_f, axis=1),
            jnp.sum(keep_rate * alpha * hidden_f * proj, axis=1),
            jnp.sum(alpha * alpha * proj * proj, axis=1),
        ),
        "grp",
    )
    proj_rs = lax.rsqrt(moments[0] / D + EPS)[:, None]
    cross_sum = moments[2][:, None]
    alpha_sum = moments[3][:, None]
    mix_mean = (moments[1][:, None] + 2.0 * proj_rs * cross_sum + proj_rs * proj_rs * alpha_sum) / D
    mix_rs = lax.rsqrt(mix_mean + EPS)
    mixed = hidden_f + alpha * (proj * proj_rs - hidden_f)
    new_hidden = (mixed * mix_rs).astype(jnp.bfloat16)
    grad_out = out_grad.astype(jnp.float32)
    grad_sums = packed_total(
        (
            jnp.sum(grad_out * keep_rate * hidden_f, axis=1),
            jnp.sum(grad_out * alpha * proj, axis=1),
        ),
        "grp",
    )
    grad_mean = (grad_sums[0][:, None] + proj_rs * grad_sums[1][:, None]) / D
    grad_mix = mix_rs * (grad_out - mixed * mix_rs * mix_rs * grad_mean)
    grad_pn = grad_mix * alpha
    proj_mean = (
        mix_rs * grad_sums[1][:, None]
        - mix_rs * mix_rs * mix_rs * grad_mean * (cross_sum + proj_rs * alpha_sum)
    ) / D
    grad_res = grad_mix * keep_rate
    grad_proj = proj_rs * (grad_pn - proj * proj_rs * proj_rs * proj_mean)
    grad_proj_b = grad_proj.astype(jnp.bfloat16)
    grad_attn_parts = contract_last(grad_proj_b, weight_o)
    grad_attn = summed_on_arrival(grad_attn_parts, "grp", 1).astype(jnp.bfloat16)
    grad_q, grad_k, grad_v = lax.map(
        head_backward, (q_heads, k_heads, v_heads, split_heads(grad_attn))
    )
    grad_values = collect(join_heads(grad_v), "grp", 1)
    grad_hidden = (
        grad_res + jnp.dot(grad_values, weight_v, preferred_element_type=jnp.float32)
    ).astype(jnp.bfloat16)
    owned = summed_rows(
        jnp.concatenate(
            (contract_first(grad_values, hidden), contract_first(attn_all, grad_proj_b)), axis=1
        ),
        ("fsdp_0", "fsdp_1", "fsdp_2"),
        "fsdp_3",
        0,
    )
    gw_v_own = owned[:, :half_width]
    gw_o_own = owned[:, half_width:]
    row_dot = packed_total(
        (jnp.sum(gw_v_own * unit_v, axis=1), jnp.sum(gw_o_own * unit_o, axis=1)), "grp"
    )
    grad_w_value = (gw_v_own - unit_v * row_dot[0][:, None]) / norm_v
    grad_w_out = (gw_o_own - unit_o * row_dot[1][:, None]) / norm_o
    return (
        new_hidden,
        grad_hidden,
        join_heads(grad_q),
        join_heads(grad_k),
        grad_w_value,
        grad_w_out,
    )


def solution(mesh):
    torus = Mesh(
        mesh.devices.reshape(2, 4, 4, 2, mesh.shape["grp"]),
        ("fsdp_0", "fsdp_1", "fsdp_2", "fsdp_3", "grp"),
    )
    placed = (
        P(FSDP, "grp"),
        P(FSDP, "grp"),
        P(FSDP, "grp"),
        P(FSDP, "grp"),
        P(FSDP, "grp"),
        P("grp"),
        P(FSDP, "grp"),
    )
    return jax.shard_map(
        shards,
        mesh=torus,
        in_specs=placed,
        out_specs=(
            P(FSDP, "grp"),
            P(FSDP, "grp"),
            P(FSDP, "grp"),
            P(FSDP, "grp"),
            P(FSDP, "grp"),
            P(FSDP, "grp"),
        ),
        check_vma=False,
    )
```

profile of v0, /device:TPU:6, one launch (start us, length us, event | category | flops | bytes accessed | tf_op | source)
XLA Modules:
  0.0 652.1 jit_solution(13862439651871433867)
XLA Ops:
  8.4 6.3 all_to_all.44
  17.4 114.7 %all-gather.2.cloned.1.call-done = bf16[1536,3072]{1,0:T(8,128)(2,1)} async-done(((bf16[24,3072]{1,0:T(8,128)(2,1)}), bf16[1536,3072]{1,0:T(8,128)(2,1)}) %all-gather.2.cloned.1.call-update) | async-done | bytes 9437200 | tf_op jit(solution)/shard_map/all_gather | solution.py:41
  132.1 7.2 %fusion.47 = f32[1536,512]{1,0:T(8,128)} fusion(bf16[512,1536]{1,0:T(8,128)(2,1)} %param.11, bf16[1536,3072]{1,0:T(8,128)(2,1)} %all-gather.2.cloned.1.call-done), kind=kOutput, calls=%fused_computation.74 | convolution fusion | flops 2415919104 | bytes 9437184 | tf_op jit(solution)/shard_map/dot_general | solution.py:75
  139.3 4.8 all-to-all-start.1
  144.1 2.3 copy.89
  146.4 2.3 copy.92
  148.7 2.3 copy.90
  151.0 2.3 copy.93
  153.3 25.8 %all-to-all-done.1 = f32[2,512,768]{1,2,0:T(8,128)S(1)} async-done(((f32[2,512,768]{1,2,0:T(8,128)}), f32[2,512,768]{1,2,0:T(8,128)S(1)}, u32[]{:S(2)}, u32[]{:S(2)}) %all-to-all-start.1) | async-done | bytes 3145760 | tf_op jit(solution)/shard_map/all_to_all | solution.py:51
  179.1 1.4 reduce_sum.174
  180.5 1.5 copy.94
  182.1 12.2 %while.24 = (s32[]{:T(128)}, bf16[6,512,128]{1,2,0:T(8,128)(2,1)S(1)}, bf16[6,512,128]{2,1,0:T(8,128)(2,1)}, bf16[6,512,128]{2,1,0:T(8,128)(2,1)}, bf16[6,512,128]{2,1,0:T(8,128)(2,1)S(1)}, /*index=5*/s32[]{:T(128)}) while((s32[]{:T(128)}, bf16[6,512,128]{1,2,0:T(8,128)(2,1)S(1)}, bf16[6,512,128]{2,1,0:T(8,128)(2,1)}, ...), condition=%wide.region_7.8_spmd, body=%wide.region_4.7_spmd.sunk | while | flops 136641536 | bytes 4205653 | solution.py:149
  182.1 1.3 fusion.113
  184.1 1.3 fusion.113
  186.1 1.3 fusion.113
  188.2 1.3 fusion.113
  190.2 1.3 fusion.113
  192.2 1.3 fusion.113
  194.3 1.3 broadcast_in_dim.40
  195.7 6.9 %all-to-all-start.2 = ((bf16[2,512,768]{1,2,0:T(8,128)(2,1)}), bf16[2,512,768]{1,2,0:T(8,128)(2,1)S(1)}, u32[]{:S(2)}, u32[]{:S(2)}) async-start(bf16[2,512,768]{1,2,0:T(8,128)(2,1)} %broadcast_in_dim.40), calls=%async_computation.2 | async-start | bytes 3145728 | tf_op jit(solution)/shard_map/all_to_all | solution.py:17
  202.6 17.3 %all-to-all-done.2 = bf16[2,512,768]{1,2,0:T(8,128)(2,1)S(1)} async-done(((bf16[2,512,768]{1,2,0:T(8,128)(2,1)}), bf16[2,512,768]{1,2,0:T(8,128)(2,1)S(1)}, u32[]{:S(2)}, u32[]{:S(2)}) %all-to-all-start.2) | async-done | bytes 1572896 | tf_op jit(solution)/shard_map/all_to_all | solution.py:17
  221.0 8.4 %fusion.54 = (f32[512]{0:T(512)S(1)}, f32[512]{0:T(512)S(1)}, f32[512]{0:T(512)S(1)}, f32[512]{0:T(512)S(1)}, f32[512]{0:T(512)S(1)}, /*index=5*/f32[512]{0:T(512)S(1)}, f32[512,1536]{1,0:T(8,128)S(1)}) fusion(bf16[512,1536]{1,0:T(8,128)(2,1)} %param.17, f32[1536]{0:T(1024)S(1)} %copy-done.10, f32[1536]{0:T(1024)S(1)} %get-tuple-element.225, ...), kind=kOutput, calls=%fused_computation.79 | convolution fusion | flops 2430858240 | bytes 12625920 | tf_op jit(solution)/shard_map/dot_general | solution.py:151
  230.1 6.5 all-to-all-start.4
  236.6 1.8 all-to-all-done.4
  239.0 6.7 %all-to-all-start.3 = ((f32[2,1,2048]{2,1,0:T(1,128)}), f32[2,1,2048]{2,1,0:T(1,128)S(1)}, u32[]{:S(2)}, u32[]{:S(2)}) async-start(f32[2,1,2048]{2,1,0:T(1,128)} %broadcast_in_dim.41), calls=%async_computation.3 | async-start | bytes 32768 | tf_op jit(solution)/shard_map/all_to_all | solution.py:17
  245.7 2.0 all-to-all-done.3
  247.8 4.4 multiply_convert_fusion.1
  252.2 5.1 fusion.41
  257.5 36.9 %all_to_all.45 = f32[2,512,768]{2,1,0:T(8,128)S(1)} all-to-all(f32[2,512,768]{2,1,0:T(8,128)S(1)} %bitcast.142), channel_id=1, replica_groups=mesh['fsdp_0'=2,'fsdp_1'=4,'fsdp_2'=4,'fsdp_3'=2,'grp'=2] {'grp'}, dimensions={0} | all-to-all | bytes 6291456 | tf_op jit(solution)/shard_map/all_to_all | solution.py:51
  294.5 1.3 reduce_sum.183
  295.8 2.3 copy.100
  299.2 47.0 %while.25 = (s32[]{:T(128)}, bf16[6,512,128]{1,2,0:T(8,128)(2,1)S(1)}, bf16[6,512,128]{1,2,0:T(8,128)(2,1)S(1)}, bf16[6,512,128]{1,2,0:T(8,128)(2,1)}, bf16[6,51...) while((s32[]{:T(128)}, ...), condition=%wide.region_21.22_spmd, body=%wide.region_17.21_spmd.sunk | while | flops 340589056 | bytes 11821177 | solution.py:190
  299.2 1.3 fusion.122
  302.1 1.3 multiply_reduce_fusion.5
  304.8 1.3 fusion.124
  307.0 1.3 fusion.122
  308.5 1.2 fusion.125
  309.9 1.3 multiply_reduce_fusion.5
  312.6 1.3 fusion.124
  314.9 1.3 fusion.122
  317.7 1.3 multiply_reduce_fusion.5
  320.5 1.3 fusion.124
  322.7 1.3 fusion.122
  324.2 1.2 fusion.125
  325.5 1.3 multiply_reduce_fusion.5
  328.3 1.3 fusion.124
  330.5 1.3 fusion.122
  333.4 1.3 multiply_reduce_fusion.5
  336.1 1.3 fusion.124
  338.4 1.3 fusion.122
  341.2 1.3 multiply_reduce_fusion.5
  344.0 1.3 fusion.124
  346.2 2.4 broadcast_in_dim.47
  348.6 7.8 %all-to-all-start.6 = ((bf16[2,512,768]{1,2,0:T(8,128)(2,1)}), bf16[2,512,768]{1,2,0:T(8,128)(2,1)}, u32[]{:S(2)}, u32[]{:S(2)}) async-start(bf16[2,512,768]{1,2,0:T(8,128)(2,1)} %broadcast_in_dim.47), calls=%async_computation.6 | async-start | bytes 3145728 | tf_op jit(solution)/shard_map/all_to_all | solution.py:17
  356.4 8.3 %fusion.86 = f32[1536,1536]{0,1:T(8,128)} fusion(bf16[512,1536]{0,1:T(8,128)(2,1)} %bitcast.153, bf16[512,1536]{1,0:T(8,128)(2,1)} %copy-done.4), kind=kOutput, calls=%fused_computation.133 | convolution fusion | flops 2415919104 | bytes 12582912 | tf_op jit(solution)/shard_map/dot_general | solution.py:81
  364.7 5.1 all-to-all-done.6
  369.8 4.2 fusion.85
  374.0 7.2 %pad_maximum_fusion = f32[1536,3072]{0,1:T(8,128)} fusion(f32[1536,1536]{0,1:T(8,128)S(1)} %copy-done, f32[1536,1536]{0,1:T(8,128)S(1)} %fusion.85), kind=kLoop, calls=%fused_computation.57 | loop fusion | flops 4718592 | bytes 37748736 | tf_op jit(solution)/shard_map/concatenate | solution.py:198
  381.2 18.7 %copy.108 = f32[1536,3072]{1,0:T(8,128)} copy(f32[1536,3072]{0,1:T(8,128)} %pad_maximum_fusion) | data formatting | bytes 37748736 | tf_op jit(solution)/shard_map/concatenate | solution.py:198
  399.9 12.8 %copy.109 = f32[2,32,24,3072]{3,2,1,0:T(8,128)} copy(f32[2,32,24,3072]{3,2,0,1:T(8,128)} %bitcast.141) | data formatting | bytes 37748736 | tf_op jit(solution)/shard_map/transpose | solution.py:69
  412.8 29.1 %reduce-scatter.3.cloned.1.call-done = f32[32,24,3072]{2,1,0:T(8,128)} async-done(((f32[64,24,3072]{2,1,0:T(8,128)}), f32[32,24,3072]{2,1,0:T(8,128)}) %reduce-scatter.3.cloned.1.call-update) | async-done | bytes 9437200 | tf_op jit(solution)/shard_map/reduce_scatter | solution.py:70
  444.3 184.6 %reduce-scatter.5.cloned.1.call-done = f32[1,24,3072]{2,1,0:T(8,128)} async-done(((f32[32,24,3072]{2,1,0:T(8,128)}), f32[1,24,3072]{2,1,0:T(8,128)}) %reduce-scatter.5.cloned.1.call-update) | async-done | bytes 294928 | tf_op jit(solution)/shard_map/reduce_scatter | solution.py:71
  630.8 4.8 all-to-all-start.7
  635.6 9.1 %fusion.62 = bf16[512,1536]{1,0:T(8,128)(2,1)} fusion(bf16[512,1536]{0,1:T(8,128)(2,1)} %bitcast.34, bf16[1536,3072]{1,0:T(8,128)(2,1)} %all-gather.2.cloned.1.call-done, bf16[512,1536]{1,0:T(8,128)(2,1)S(1)} %copy-done.2, f32[512]{0:T(512)S(1)} %get-tuple-element.211, f32[1536]{0:T(1024)S(1)} %get-tuple-element.228, f32[512]{0:T(512)S(1)} %get-tuple-element.226, ...), kind=kOutput, calls=%fused_computation.90 | convolution fusion | flops 2426929152 | bytes 14174208 | tf_op jit(solution)/shard_map/dot_general | solution.py:195
  (134 shorter events, 38.5 us)
Async XLA Ops:
  7.2 125.0 %all-gather.2.cloned.1.call-start = ((), (), s32[]{:S(2)}) async-start(), calls=%async_computation.10 | async-start | bytes 9584640 | tf_op jit(solution)/shard_map/all_gather | solution.py:41
  139.3 39.8 %all-to-all-start.1 = ((f32[2,512,768]{1,2,0:T(8,128)}), f32[2,512,768]{1,2,0:T(8,128)S(1)}, u32[]{:S(2)}, u32[]{:S(2)}) async-start(f32[2,512,768]{1,2,0:T(8,128)} %bitcast.143), calls=%async_computation.1 | async-start | bytes 6291456 | tf_op jit(solution)/shard_map/all_to_all | solution.py:51
  194.2 1.4 copy-start.9
  194.3 8.3 %copy-start.10 = (f32[1536]{0:T(1024)S(1)}, f32[1536]{0:T(1024)}, u32[]{:S(2)}) copy-start(f32[1536]{0:T(1024)} %param.16) | copy-start | bytes 18436
  195.7 24.2 %all-to-all-start.2 = ((bf16[2,512,768]{1,2,0:T(8,128)(2,1)}), bf16[2,512,768]{1,2,0:T(8,128)(2,1)S(1)}, u32[]{:S(2)}, u32[]{:S(2)}) async-start(bf16[2,512,768]{1,2,0:T(8,128)(2,1)} %broadcast_in_dim.40), calls=%async_computation.2 | async-start | bytes 3145728 | tf_op jit(solution)/shard_map/all_to_all | solution.py:17
  219.9 1.1 copy-start.5
  229.4 22.7 %copy-start.1 = (f32[512,1536]{1,0:T(8,128)}, f32[512,1536]{1,0:T(8,128)S(1)}, u32[]{:S(2)}) copy-start(f32[512,1536]{1,0:T(8,128)S(1)} %get-tuple-element.234) | copy-start | bytes 9437188
  230.1 8.3 %all-to-all-start.4 = ((f32[2,1,1024]{2,1,0:T(1,128)}), f32[2,1,1024]{2,1,0:T(1,128)S(1)}, u32[]{:S(2)}, u32[]{:S(2)}) async-start(f32[2,1,1024]{2,1,0:T(1,128)} %broadcast_in_dim.42), calls=%async_computation.4 | async-start | bytes 16384 | tf_op jit(solution)/shard_map/all_to_all | solution.py:17
  239.0 8.8 %all-to-all-start.3 = ((f32[2,1,2048]{2,1,0:T(1,128)}), f32[2,1,2048]{2,1,0:T(1,128)S(1)}, u32[]{:S(2)}, u32[]{:S(2)}) async-start(f32[2,1,2048]{2,1,0:T(1,128)} %broadcast_in_dim.41), calls=%async_computation.3 | async-start | bytes 32768 | tf_op jit(solution)/shard_map/all_to_all | solution.py:17
  252.2 5.1 copy-start.4
  348.6 21.2 %all-to-all-start.6 = ((bf16[2,512,768]{1,2,0:T(8,128)(2,1)}), bf16[2,512,768]{1,2,0:T(8,128)(2,1)}, u32[]{:S(2)}, u32[]{:S(2)}) async-start(bf16[2,512,768]{1,2,0:T(8,128)(2,1)} %broadcast_in_dim.47), calls=%async_computation.6 | async-start | bytes 3145728 | tf_op jit(solution)/shard_map/all_to_all | solution.py:17
  356.4 13.4 %copy-start.3 = (bf16[512,1536]{1,0:T(8,128)(2,1)S(1)}, bf16[512,1536]{1,0:T(8,128)(2,1)}, u32[]{:S(2)}) copy-start(bf16[512,1536]{1,0:T(8,128)(2,1)} %param.11) | copy-start | bytes 4718596
  356.4 85.5 %reduce-scatter.3.cloned.1.call-start = ((), (), s32[]{:S(2)}) async-start(), calls=%async_computation.11 | async-start | bytes 28311552 | tf_op jit(solution)/shard_map/reduce_scatter | solution.py:70
  369.8 4.3 copy-start
  412.8 216.1 %reduce-scatter.5.cloned.1.call-start = ((), (), s32[]{:S(2)}) async-start(), calls=%async_computation.12 | async-start | bytes 9732096 | tf_op jit(solution)/shard_map/reduce_scatter | solution.py:71
  442.0 186.9 %copy-start.6 = (bf16[24,1536]{1,0:T(8,128)(2,1)S(1)}, bf16[24,1536]{1,0:T(8,128)(2,1)}, u32[]{:S(2)}) copy-start(bf16[24,1536]{1,0:T(8,128)(2,1)} %param.14) | copy-start | bytes 221188
  442.0 186.9 %copy-start.7 = (bf16[24,1536]{1,0:T(8,128)(2,1)S(1)}, bf16[24,1536]{1,0:T(8,128)(2,1)}, u32[]{:S(2)}) copy-start(bf16[24,1536]{1,0:T(8,128)(2,1)} %param.15) | copy-start | bytes 221188
  442.0 193.6 %copy-start.2 = (bf16[512,1536]{1,0:T(8,128)(2,1)S(1)}, bf16[512,1536]{1,0:T(8,128)(2,1)}, u32[]{:S(2)}) copy-start(bf16[512,1536]{1,0:T(8,128)(2,1)} %param.17) | copy-start | bytes 4718596
  630.8 13.9 %all-to-all-start.7 = ((f32[2,1,48]{2,1,0:T(1,128)}), f32[2,1,48]{2,1,0:T(1,128)S(1)}, u32[]{:S(2)}, u32[]{:S(2)}) async-start(f32[2,1,48]{2,1,0:T(1,128)} %broadcast_in_dim.48), calls=%async_computation.9 | async-start | bytes 2048 | tf_op jit(solution)/shard_map/all_to_all | solution.py:17
  635.6 9.2 %copy-start.8 = (f32[1,24,3072]{2,1,0:T(8,128)S(1)}, f32[1,24,3072]{2,1,0:T(8,128)}, u32[]{:S(2)}) copy-start(f32[1,24,3072]{2,1,0:T(8,128)} %reduce-scatter.5.cloned.1.call-done) | copy-start | bytes 884740
Sparse Core Ops, SparseCore 0:
  17.6 114.5 all-gather.1
  412.9 29.0 reduce-scatter.2
  444.4 184.4 reduce-scatter.4
where the time goes:
time: 654 us; the launch traced here: 652 us
  waiting for transfers between devices  380 us (58%)
  matrix products  89.9 us (14%)
  local copies, waits for them, and re-layouts  62 us (9%)
  blocking collectives  43.3 us (7%)
  starting transfers between devices  37.6 us (6%)
  other arithmetic  24.3 us (4%)
  between operations  13.9 us (2%)
    reduce_scatter x1, waiting for transfers between devices, summed_rows(): return lax.psum_scatter(tiles, chips, scatter_dimension=0, tiled=True)[0]  185 us
    all_gather x1, waiting for transfers between devices, sent_together(): lax.all_gather(both, axis, axis=dim, tiled=True)  115 us
    all_to_all x1, blocking collectives, summed_on_arrival(): lax.all_to_all(tiles, axis, split_axis=0, concat_axis=0, tiled=True)  36.9 us
    dot_general x20, matrix products, contract_last(): lax.dot_general(left, right, (((1,), (1,)), ((), ())), preferred_element_...  35.3 us
    all_to_all x5, starting transfers between devices, from_everyone(): lax.all_to_all(jnp.broadcast_to(value[None], (count, *value.shape)), axis...  32.7 us
    reduce_scatter x1, waiting for transfers between devices, summed_rows(): tiles = lax.psum_scatter(tiles, core, scatter_dimension=0, tiled=True)  29.1 us
    dot_general x14, matrix products, contract_first(): lax.dot_general(left, right, (((0,), (0,)), ((), ())), preferred_element_...  27.2 us
    all_to_all x5, waiting for transfers between devices, from_everyone(): lax.all_to_all(jnp.broadcast_to(value[None], (count, *value.shape)), axis...  26.2 us
  transfers between devices with their start and end apart: 9, of which 8 were waited for; matrix products, arithmetic and copies ran while one was open for 4% of the time, Pallas kernels for 0%

commit v1 on v0

v1 whole, which is shorter than its diff:
```python
import jax
import jax.numpy as jnp
from jax import lax
from jax.experimental import pallas as pl
from jax.experimental.pallas import tpu as pltpu
from jax.sharding import Mesh
from jax.sharding import PartitionSpec as P

D = 3072
EPS = 1e-06
AXES = ("fsdp_0", "fsdp_1", "fsdp_2", "fsdp_3", "grp")
FSDP = AXES[:4]
SCALE = 128 ** (-0.5)
F32 = jnp.float32
BF16 = jnp.bfloat16
MESH = pl.DeviceIdType.MESH


def nt(a, b):
    return lax.dot_general(a, b, (((1,), (1,)), ((), ())), preferred_element_type=F32)


def tn(a, b):
    return lax.dot_general(a, b, (((0,), (0,)), ((), ())), preferred_element_type=F32)


def nn(a, b):
    return lax.dot_general(a, b, (((1,), (0,)), ((), ())), preferred_element_type=F32)


def lanes(start, size):
    return pl.ds(pl.multiple_of(start, 128), size)


def kernel(
    hid_h, q_h, k_h, wv_h, wo_h, al, og_h,
    nh_h, gh_h, gq_h, gk_h, gwv_h, gwo_h,
    hid, q, k, og, wraw, unit, nrm, nsend, nrecv, usr, W,
    vsend, vrecv, vown, V, Pr, ATT, proj, gpb, mom, msend, mrecv,
    garecv, GA, gsb, gq, gk, GV, gss, gsr, RSA, r1b, S1, r2b, xk, xs, xr, fin, gown, rds, rdr,
    in_m, out_m, nm_s, nm_r, us_s, us_r, ax_s, ax_r, p1_s, p1_r, p2_s, p2_r, sb_s, sb_r,
    ex_s, ex_r, gs_s, gs_r, r1_s, r1_r, r2_s, r2_r, rx_s, rx_r, fd_s, fd_r,
):
    x, y, z, c, g = (lax.axis_index(a) for a in AXES)
    oc = 1 - c
    og_ = 1 - g

    def ring(v, d):
        return lax.rem(v + d, 4)

    sib = (x, y, z, oc, g)
    mate = (x, y, z, c, og_)
    xdev = (1 - x, y, z, c, g)

    def ydev(d):
        return (x, ring(y, d), z, c, g)

    def zdev(d):
        return (x, y, ring(z, d), c, g)

    def rc(src, dst, ss, rs, dev):
        return pltpu.make_async_remote_copy(
            src_ref=src, dst_ref=dst, send_sem=ss, recv_sem=rs, device_id=dev, device_id_type=MESH
        )

    ins = [
        pltpu.make_async_copy(wv_h, wraw.at[0], in_m.at[0]),
        pltpu.make_async_copy(wo_h, wraw.at[1], in_m.at[1]),
        pltpu.make_async_copy(q_h, q, in_m.at[2]),
        pltpu.make_async_copy(k_h, k, in_m.at[3]),
        pltpu.make_async_copy(hid_h, hid, in_m.at[4]),
        pltpu.make_async_copy(og_h, og, in_m.at[5]),
    ]
    for cp in ins:
        cp.start()

    barrier = pltpu.get_barrier_semaphore()
    peers = [sib, mate, xdev] + [ydev(d) for d in (1, 2, 3)] + [zdev(d) for d in (1, 2, 3)]
    for dev in peers:
        pl.semaphore_signal(barrier, inc=1, device_id=dev, device_id_type=MESH)

    gsb[...] = jnp.zeros_like(gsb)
    ins[0].wait()
    ins[1].wait()
    for w in range(2):
        rows = wraw[w].astype(F32)
        nsend[w] = jnp.broadcast_to(jnp.sum(rows * rows, axis=1, keepdims=True), (24, 128))
    pl.semaphore_wait(barrier, len(peers))
    ncp = rc(nsend, nrecv, nm_s.at[0], nm_r.at[0], mate)
    ncp.start()

    def probs(first, last):
        def one(h, carry):
            hc = lanes(128 * h, 128)
            for r in range(4):
                n = 128 * (r + 1)
                rr = pl.ds(128 * r, 128)
                s = nt(q[rr, hc], k[pl.ds(0, n), hc]) * SCALE
                row = lax.broadcasted_iota(jnp.int32, (128, n), 0) + 128 * r
                col = lax.broadcasted_iota(jnp.int32, (128, n), 1)
                s = jnp.where(row >= col, s, -1e30)
                e = jnp.exp(s - jnp.max(s, axis=1, keepdims=True))
                Pr[h, rr, pl.ds(0, n)] = e / jnp.sum(e, axis=1, keepdims=True)
                if r < 3:
                    Pr[h, rr, pl.ds(n, 512 - n)] = jnp.zeros((128, 512 - n), F32)
            return carry

        lax.fori_loop(first, last, one, 0)

    ins[2].wait()
    ins[3].wait()
    probs(0, 1)

    ncp.wait()
    for w in range(2):
        norm = jnp.sqrt(nsend[w] + nrecv[w] + EPS)
        nrm[w] = norm
        unit[w] = wraw[w].astype(F32) / norm[:, :1]
    ucp = rc(unit.at[:, :, lanes(768 * oc, 768)], usr, us_s.at[0], us_r.at[0], sib)
    ucp.start()
    ucp.wait()
    for w in range(2):
        mine = unit[w, :, lanes(768 * c, 768)]
        other = usr[w]
        low = jnp.where(c == 0, mine, other)
        high = jnp.where(c == 0, other, mine)
        W[w, x, y, z, :, lanes(768 * c, 768)] = jnp.concatenate([low, high], axis=0).astype(BF16)

    def cols(s):
        return lanes(768 * c + 384 * s, 384)

    axs = []
    for w in range(2):
        blk = W.at[w, x, y, z, :, lanes(768 * c, 768)]
        axs.append(rc(blk, blk, ax_s.at[w], ax_r.at[w], xdev))
    p1 = {}
    p2 = {}
    sbc = {}
    for w in range(2):
        for s in range(2):
            for d in (1, 2, 3):
                blk = W.at[w, :, y, z, :, cols(s)]
                p1[w, s, d] = rc(
                    blk, blk, p1_s.at[w, s, d - 1], p1_r.at[w, s, d - 1], ydev(d) if s == 0 else zdev(d)
                )
                for e in range(4):
                    if s == 0:
                        blk = W.at[w, :, ring(y, 4 - e), z, :, cols(s)]
                        dev = zdev(d)
                    else:
                        blk = W.at[w, :, y, ring(z, 4 - e), :, cols(s)]
                        dev = ydev(d)
                    p2[w, s, e, d] = rc(blk, blk, p2_s.at[w, s, e, d - 1], p2_r.at[w, s, e, d - 1], dev)
            for e in range(4):
                if s == 0:
                    blk = W.at[w, :, :, ring(z, 4 - e), :, cols(s)]
                else:
                    blk = W.at[w, :, ring(y, 4 - e), :, :, cols(s)]
                sbc[w, s, e] = rc(blk, blk, sb_s.at[w, s, e], sb_r.at[w, s, e], sib)

    def gather_first(w):
        axs[w].wait()
        for d in (1, 2, 3):
            for s in range(2):
                p1[w, s, d].start()
        for d in (1, 2, 3):
            for s in range(2):
                p2[w, s, 0, d].start()

    def gather_second(w):
        for d in (1, 2, 3):
            for s in range(2):
                p1[w, s, d].wait()
                for e in (1, 2, 3):
                    p2[w, s, d, e].start()
        for s in range(2):
            sbc[w, s, 0].start()

    def gather_last(w):
        for d in (1, 2, 3):
            for s in range(2):
                for e in range(4):
                    p2[w, s, e, d].wait()
                sbc[w, s, d].start()
        for s in range(2):
            for e in range(4):
                sbc[w, s, e].wait()

    axs[0].start()
    axs[1].start()
    probs(1, 2)
    gather_first(0)
    probs(2, 3)
    gather_second(0)
    gather_first(1)
    probs(3, 6)
    ins[4].wait()
    gather_last(0)

    exs = {}

    def exchange(kind, j, src, dst):
        cp = rc(src, dst, ex_s.at[kind, j], ex_r.at[kind, j], mate)
        cp.start()
        exs[kind, j] = cp

    for j in range(2):
        part = nt(hid[...], W[0, og_, 2 * j : 2 * j + 2].reshape(384, 1536))
        vsend[j] = part.astype(BF16)
        exchange(0, j, vsend.at[j], vrecv.at[j])
    for j in range(2):
        vown[j] = nt(hid[...], W[0, g, 2 * j : 2 * j + 2].reshape(384, 1536))
    gather_second(1)
    for j in range(2):
        exs[0, j].wait()
        V[j] = (vown[j] + vrecv[j].astype(F32)).astype(BF16)

        def fwd(i, carry):
            hc = lanes(128 * i, 128)
            vals = V[j, :, hc]
            ATT[:, lanes(768 * g + 384 * j + 128 * i, 128)] = nn(
                Pr[3 * j + i].astype(BF16), vals
            ).astype(BF16)
            return carry

        lax.fori_loop(0, 3, fwd, 0)
        blk = ATT.at[:, lanes(768 * g + 384 * j, 384)]
        exchange(1, j, blk, blk)
    gather_last(1)

    def proj_own(n, carry):
        nc = lanes(384 * n, 384)
        proj[:, nc] = nn(ATT[:, lanes(768 * g, 768)], W[1, g, :, :, :, nc].reshape(768, 384))
        return carry

    lax.fori_loop(0, 4, proj_own, 0)
    for j in range(2):
        exs[1, j].wait()

        def proj_more(n, carry):
            nc = lanes(384 * n, 384)
            proj[:, nc] += nn(
                ATT[:, lanes(768 * og_ + 384 * j, 384)],
                W[1, og_, 2 * j : 2 * j + 2, :, :, nc].reshape(384, 384),
            )
            return carry

        lax.fori_loop(0, 4, proj_more, 0)

    ins[5].wait()
    lane = lax.broadcasted_iota(jnp.int32, (16, 128), 1)

    def sums(i, carry):
        rr = pl.ds(pl.multiple_of(16 * i, 16), 16)
        a = al[...]
        kr = 1.0 - a
        p = proj[rr, :]
        hf = hid[rr, :].astype(F32)
        go = og[rr, :].astype(F32)
        kh = kr * hf
        ap = a * p
        parts = (p * p, kh * kh, kh * ap, ap * ap, go * kh, go * ap)
        acc = jnp.zeros((16, 128), F32)
        for j, v in enumerate(parts):
            acc = jnp.where(lane == j, jnp.sum(v, axis=1, keepdims=True), acc)
        mom[rr, :] = acc
        return carry

    lax.fori_loop(0, 32, sums, 0)
    msend[...] = mom[...].T[:8]
    mcp = rc(msend, mrecv.at[pl.ds(0, 8)], nm_s.at[1], nm_r.at[1], mate)
    mrecv[pl.ds(8, 120), :] = jnp.zeros((120, 512), F32)
    mcp.start()
    mcp.wait()
    mom[...] = mom[...] + mrecv[...].T

    def apply(i, carry):
        rr = pl.ds(pl.multiple_of(16 * i, 16), 16)
        a = al[...]
        kr = 1.0 - a
        m = mom[rr, :]
        p = proj[rr, :]
        hf = hid[rr, :].astype(F32)
        go = og[rr, :].astype(F32)
        pr = lax.rsqrt(m[:, 0:1] / D + EPS)
        mm = (m[:, 1:2] + 2.0 * pr * m[:, 2:3] + pr * pr * m[:, 3:4]) / D
        mr = lax.rsqrt(mm + EPS)
        gm = (m[:, 4:5] + pr * m[:, 5:6]) / D
        pm = (mr * m[:, 5:6] - mr * mr * mr * gm * (m[:, 2:3] + pr * m[:, 3:4])) / D
        mixed = hf + a * (p * pr - hf)
        og[rr, :] = (mixed * mr).astype(BF16)
        gmix = mr * (go - mixed * (mr * mr * gm))
        proj[rr, :] = gmix * kr
        gpb[rr, :] = (pr * (gmix * a - p * (pr * pr * pm))).astype(BF16)
        return carry

    lax.fori_loop(0, 32, apply, 0)
    outs = [pltpu.make_async_copy(og, nh_h, out_m.at[0])]
    outs[0].start()

    for j in range(2):
        vsend[j] = nt(gpb[...], W[1, og_, 2 * j : 2 * j + 2].reshape(384, 1536)).astype(BF16)
        exchange(2, j, vsend.at[j], garecv.at[j])

    gsc = {}
    r1c = {}
    r2c = {}

    def half(p):
        return g if p == 0 else og_

    def rs_partner(w, p, left, right):
        for j in range(2):
            gss[p, pl.ds(384 * j, 384), :] = tn(
                left[:, lanes(768 * half(p) + 384 * j, 384)], right[:, lanes(768 * oc, 768)]
            ).astype(BF16)
            rr = pl.ds(384 * j, 384)
            gsc[w, p, j] = rc(
                gss.at[p, rr], gsr.at[w, p, rr], gs_s.at[w, p, j], gs_r.at[w, p, j], sib
            )
            gsc[w, p, j].start()

    def rs_own(w, p, left, right):
        for j in range(2):
            part = tn(left[:, lanes(768 * half(p) + 384 * j, 384)], right[:, lanes(768 * c, 768)])
            gsc[w, p, j].wait()
            total = part + gsr[w, p, pl.ds(384 * j, 384), :].astype(F32)
            RSA[p, 2 * j : 2 * j + 2] = total.astype(BF16).reshape(2, 4, 48, 768)
        for d in (1, 2, 3):
            r1c[w, p, 0, d] = rc(
                RSA.at[p, :, ring(z, d), :, pl.ds(0, 384)], r1b.at[w, p, 0, d - 1],
                r1_s.at[w, p, 0, d - 1], r1_r.at[w, p, 0, d - 1], zdev(d),
            )
            r1c[w, p, 0, d].start()
            r1c[w, p, 1, d] = rc(
                RSA.at[p, ring(y, d), :, :, pl.ds(384, 384)], r1b.at[w, p, 1, d - 1],
                r1_s.at[w, p, 1, d - 1], r1_r.at[w, p, 1, d - 1], ydev(d),
            )
            r1c[w, p, 1, d].start()

    def rs_second(w, p):
        for s in range(2):
            for d in (1, 2, 3):
                r1c[w, p, s, d].wait()
            for b in range(4):
                if s == 0:
                    acc = RSA[p, b, z, :, pl.ds(0, 384)].astype(F32)
                else:
                    acc = RSA[p, y, b, :, pl.ds(384, 384)].astype(F32)
                for d in range(3):
                    acc += r1b[w, p, s, d, b].astype(F32)
                S1[p, s, b] = acc.astype(BF16)
            for d in (1, 2, 3):
                at = ring(y, d) if s == 0 else ring(z, d)
                dev = ydev(d) if s == 0 else zdev(d)
                r2c[w, p, s, d] = rc(
                    S1.at[p, s, at], r2b.at[w, p, s, d - 1],
                    r2_s.at[w, p, s, d - 1], r2_r.at[w, p, s, d - 1], dev,
                )
                r2c[w, p, s, d].start()

    def rs_third(w, p):
        for s in range(2):
            for d in (1, 2, 3):
                r2c[w, p, s, d].wait()
            acc = S1[p, s, y if s == 0 else z].astype(F32)
            for d in range(3):
                acc += r2b[w, p, s, d].astype(F32)
            xk[w, p, :, pl.ds(384 * s, 384)] = acc
            xs[w, p, :, pl.ds(384 * s, 384)] = acc.astype(BF16)

    away = jnp.where(x == g, 1, 0)
    rxc = [rc(xs.at[w, away], xr.at[w], rx_s.at[w], rx_r.at[w], xdev) for w in range(2)]
    fdc = [
        rc(
            fin.at[w, pl.ds(pl.multiple_of(24 * oc, 8), 24)], gown.at[w, :, lanes(768 * c, 768)],
            fd_s.at[w], fd_r.at[w], sib,
        )
        for w in range(2)
    ]

    def rs_owner(w):
        rxc[w].wait()
        fin[w] = xk[w, 1 - away] + xr[w].astype(F32)
        gown[w, :, lanes(768 * c, 768)] = fin[w, pl.ds(pl.multiple_of(24 * c, 8), 24), :]
        fdc[w].start()

    rs_partner(1, 0, ATT, gpb)
    rs_partner(1, 1, ATT, gpb)
    for j in range(2):
        vown[j] = nt(gpb[...], W[1, g, 2 * j : 2 * j + 2].reshape(384, 1536))
    rs_own(1, 0, ATT, gpb)
    rs_own(1, 1, ATT, gpb)

    for j in range(2):
        exs[2, j].wait()
        GA[...] = (vown[j] + garecv[j].astype(F32)).astype(BF16)

        def bwd(i, carry):
            h = 3 * j + i
            hc = lanes(128 * h, 128)
            ic = lanes(128 * i, 128)
            for r in range(4):
                n = 128 * (r + 1)
                rr = pl.ds(128 * r, 128)
                gp = nt(GA[rr, ic], V[j, pl.ds(0, n), ic])
                pb = Pr[h, rr, pl.ds(0, n)]
                delta = jnp.sum(pb * gp, axis=1, keepdims=True)
                gs = (pb * (gp - delta)).astype(BF16)
                gsb[rr, pl.ds(0, n)] = gs
                gq[rr, hc] = (nn(gs, k[pl.ds(0, n), hc]) * SCALE).astype(BF16)
            gk[:, hc] = (tn(gsb[...], q[:, hc]) * SCALE).astype(BF16)
            GV[:, lanes(768 * g + 384 * j + 128 * i, 128)] = tn(
                Pr[h].astype(BF16), GA[:, ic]
            ).astype(BF16)
            return carry

        lax.fori_loop(0, 3, bwd, 0)
        blk = GV.at[:, lanes(768 * g + 384 * j, 384)]
        exchange(3, j, blk, blk)
        if j == 0:
            rs_second(1, 0)
            rs_second(1, 1)
    outs.append(pltpu.make_async_copy(gq, gq_h, out_m.at[1]))
    outs.append(pltpu.make_async_copy(gk, gk_h, out_m.at[2]))
    outs[1].start()
    outs[2].start()
    rs_third(1, 0)
    rs_third(1, 1)
    rxc[1].start()

    rs_partner(0, 0, GV, hid)
    rs_own(0, 0, GV, hid)
    rs_owner(1)
    exs[3, 0].wait()
    exs[3, 1].wait()
    rs_partner(0, 1, GV, hid)
    rs_own(0, 1, GV, hid)
    rs_second(0, 0)

    def hidden_grad(n, carry):
        nc = lanes(384 * n, 384)
        gpb[:, nc] = (proj[:, nc] + nn(GV[...], W[0, :, :, :, :, nc].reshape(1536, 384))).astype(BF16)
        return carry

    lax.fori_loop(0, 2, hidden_grad, 0)
    rs_second(0, 1)
    rs_third(0, 0)
    lax.fori_loop(2, 4, hidden_grad, 0)
    outs.append(pltpu.make_async_copy(gpb, gh_h, out_m.at[3]))
    outs[3].start()
    rs_third(0, 1)
    rxc[0].start()
    rs_owner(0)
    fdc[0].wait()
    fdc[1].wait()
    for w in range(2):
        rds[w] = jnp.broadcast_to(jnp.sum(gown[w] * unit[w], axis=1, keepdims=True), (24, 128))
    rcp = rc(rds, rdr, nm_s.at[2], nm_r.at[2], mate)
    rcp.start()
    rcp.wait()
    for w in range(2):
        dot = (rds[w] + rdr[w])[:, :1]
        gown[w] = (gown[w] - unit[w] * dot) / nrm[w][:, :1]
    outs.append(pltpu.make_async_copy(gown.at[0], gwv_h, out_m.at[4]))
    outs.append(pltpu.make_async_copy(gown.at[1], gwo_h, out_m.at[5]))
    outs[4].start()
    outs[5].start()
    for cp in outs:
        cp.wait()


def shards(hidden, queries, attn_keys, w_value, w_out, alpha, out_grad):
    vm = pltpu.VMEM
    dma = pltpu.SemaphoreType.DMA
    hbm = pl.BlockSpec(memory_space=pltpu.HBM)
    scratch = [
        vm((512, 1536), BF16), vm((512, 768), BF16), vm((512, 768), BF16), vm((512, 1536), BF16),
        vm((2, 24, 1536), BF16), vm((2, 24, 1536), F32), vm((2, 24, 128), F32),
        vm((2, 24, 128), F32), vm((2, 24, 128), F32), vm((2, 24, 768), F32),
        vm((2, 2, 4, 4, 48, 1536), BF16),
        vm((2, 512, 384), BF16), vm((2, 512, 384), BF16), vm((2, 512, 384), F32), vm((2, 512, 384), BF16),
        vm((6, 512, 512), F32), vm((512, 1536), BF16), vm((512, 1536), F32), vm((512, 1536), BF16),
        vm((512, 128), F32), vm((8, 512), F32), vm((128, 512), F32),
        vm((2, 512, 384), BF16), vm((512, 384), BF16), vm((512, 512), BF16),
        vm((512, 768), BF16), vm((512, 768), BF16), vm((512, 1536), BF16),
        vm((2, 768, 768), BF16), vm((2, 2, 768, 768), BF16), vm((2, 4, 4, 48, 768), BF16),
        vm((2, 2, 2, 3, 4, 48, 384), BF16), vm((2, 2, 4, 48, 384), BF16), vm((2, 2, 2, 3, 48, 384), BF16),
        vm((2, 2, 48, 768), F32), vm((2, 2, 48, 768), BF16), vm((2, 48, 768), BF16),
        vm((2, 48, 768), F32), vm((2, 24, 1536), F32), vm((2, 24, 128), F32), vm((2, 24, 128), F32),
        dma((6,)), dma((6,)), dma((3,)), dma((3,)), dma((1,)), dma((1,)), dma((2,)), dma((2,)),
        dma((2, 2, 3)), dma((2, 2, 3)), dma((2, 2, 4, 3)), dma((2, 2, 4, 3)), dma((2, 2, 4)), dma((2, 2, 4)),
        dma((4, 2)), dma((4, 2)), dma((2, 2, 2)), dma((2, 2, 2)),
        dma((2, 2, 2, 3)), dma((2, 2, 2, 3)), dma((2, 2, 2, 3)), dma((2, 2, 2, 3)),
        dma((2,)), dma((2,)), dma((2,)), dma((2,)),
    ]
    sds = jax.ShapeDtypeStruct
    return pl.pallas_call(
        kernel,
        out_shape=(
            sds((512, 1536), BF16), sds((512, 1536), BF16), sds((512, 768), BF16),
            sds((512, 768), BF16), sds((24, 1536), F32), sds((24, 1536), F32),
        ),
        in_specs=[hbm] * 5 + [pl.BlockSpec(memory_space=pltpu.VMEM), hbm],
        out_specs=[hbm] * 6,
        scratch_shapes=scratch,
        compiler_params=pltpu.CompilerParams(
            collective_id=0, has_side_effects=True, vmem_limit_bytes=67043328
        ),
        name="sublayer",
    )(hidden, queries, attn_keys, w_value, w_out, alpha.reshape(1, 1536), out_grad)


def solution(mesh):
    torus = Mesh(mesh.devices.reshape(2, 4, 4, 2, mesh.shape["grp"]), AXES)
    both = P(FSDP, "grp")
    return jax.shard_map(
        shards,
        mesh=torus,
        in_specs=(both, both, both, both, both, P("grp"), both),
        out_specs=(both,) * 6,
        check_vma=False,
    )
```

time: 654 us -> 177 us (0.27)
  the two profiles are of different devices: /device:TPU:6 before, /device:TPU:1 now
where the time goes in v1:
time: 177 us; the launch traced here: 176 us
  Pallas kernels  166 us (94%)
  local copies, waits for them, and re-layouts  9.37 us (5%)
    pallas_call x1, Pallas kernels, shards(): pl.pallas_call(kernel, out_shape=(sds((512, 1536), BF16), sds((512, 1536)...  166 us
    unnamed x16, local copies, waits for them, and re-layouts  8.07 us

profile of v1, /device:TPU:1, one launch (start us, length us, event | category | flops | bytes accessed | tf_op | source)
XLA Modules:
  0.0 176.2 jit_solution(15060014544510136562)
XLA Ops:
  0.6 1.3 reshape.15.al
  1.9 166.2 %sublayer.1 = (bf16[512,1536]{1,0:T(8,128)(2,1)}, bf16[512,1536]{1,0:T(8,128)(2,1)}, bf16[512,768]{1,0:T(8,128)(2,1)}, bf16[512,768]{1,0:T(8,128)(2,1)}, f32[24,1536]{1,0:T(8,128)}, /*index=5*/f32[24,1536]{1,0:T(8,128)}) custom-call(bf16[512,1536]{1,0:T(8,128)(2,1)} %hid_h.1, bf16[512,768]{1,0:T(8,128)(2,1)} %q_h.1, bf16[512,768]{1,0:T(8,128)(2,1)} %k_h.1, ...), custom_call_target="tpu_custom_call" | custom-call | tf_op jit(solution)/shard_map/sublayer/pallas_call | solution.py:498
  168.2 0.0 copy-start
  168.2 2.8 %copy.19 = bf16[512,1536]{1,0:T(8,128)(2,1)} copy(bf16[512,1536]{1,0:T(8,128)(2,1)} %get-tuple-element.12) | data formatting | bytes 3145728
  170.9 0.0 copy-done
  170.9 0.0 copy-start.2
  170.9 1.1 copy.20
  172.1 0.5 copy-done.2
  172.6 0.0 copy-start.1
  172.6 0.0 copy-start.4
  172.6 0.0 copy-start.3
  172.6 0.9 copy.21
  173.5 0.5 copy-done.1
  174.0 0.9 copy.22
  174.9 0.0 copy-done.4
  174.9 0.7 copy.23
  175.6 0.0 copy-done.3
  175.6 0.7 copy.24
Async XLA Ops:
  168.2 2.8 %copy-start = (bf16[512,1536]{1,0:T(8,128)(2,1)S(1)}, bf16[512,1536]{1,0:T(8,128)(2,1)}, u32[]{:S(2)}) copy-start(bf16[512,1536]{1,0:T(8,128)(2,1)} %get-tuple-element.13) | copy-start | bytes 4718596
  170.9 1.7 copy-start.2
  172.6 1.4 copy-start.1
  172.6 2.3 %copy-start.4 = (f32[24,1536]{1,0:T(8,128)S(1)}, f32[24,1536]{1,0:T(8,128)}, u32[]{:S(2)}) copy-start(f32[24,1536]{1,0:T(8,128)} %get-tuple-element.16) | copy-start | bytes 442372
  172.6 3.0 %copy-start.3 = (f32[24,1536]{1,0:T(8,128)S(1)}, f32[24,1536]{1,0:T(8,128)}, u32[]{:S(2)}) copy-start(f32[24,1536]{1,0:T(8,128)} %get-tuple-element.17) | copy-start | bytes 442372

commit v2 on v1

v2 whole, which is shorter than its diff:
```python
import jax
import jax.numpy as jnp
from jax import lax
from jax.experimental import pallas as pl
from jax.experimental.pallas import tpu as pltpu
from jax.sharding import Mesh
from jax.sharding import PartitionSpec as P

D = 3072
EPS = 1e-06
AXES = ("fsdp_0", "fsdp_1", "fsdp_2", "fsdp_3", "grp")
FSDP = AXES[:4]
SCALE = 128 ** (-0.5)
F32 = jnp.float32
BF16 = jnp.bfloat16
MESH = pl.DeviceIdType.MESH


def nt(a, b):
    return lax.dot_general(a, b, (((1,), (1,)), ((), ())), preferred_element_type=F32)


def tn(a, b):
    return lax.dot_general(a, b, (((0,), (0,)), ((), ())), preferred_element_type=F32)


def nn(a, b):
    return lax.dot_general(a, b, (((1,), (0,)), ((), ())), preferred_element_type=F32)


def lanes(start, size):
    return pl.ds(pl.multiple_of(start, 128), size)


def kernel(
    hid_h, q_h, k_h, wv_h, wo_h, al, og_h,
    nh_h, gh_h, gq_h, gk_h, gwv_h, gwo_h,
    hid, q, k, og, wraw, unit, nrm, nsend, nrecv, rawr, U48, W,
    vsend, vrecv, vown, V, Pr, ATT, proj, gpb, mom, msend, mrecv,
    gasend, garecv, GA, gsb, gq, gk, GV, gss, gsr, RSA, r1b, S1, r2b, xk, xs, xr, gpt, gown, rds, rdr,
    in_m, out_m, nm_s, nm_r, us_s, us_r, p1_s, p1_r, p2_s, p2_r, sb_s, sb_r,
    ex_s, ex_r, gs_s, gs_r, r1_s, r1_r, r2_s, r2_r, fd_s, fd_r,
):
    x, y, z, c, g = (lax.axis_index(a) for a in AXES)
    oc = 1 - c
    og_ = 1 - g

    def ring(v, d):
        return lax.rem(v + d, 4)

    def row(i):
        return (1 - x if i & 4 else x, y, z, oc if i & 2 else c, og_ if i & 1 else g)

    mate = row(1)
    sib = row(2)

    def ydev(d):
        return (x, ring(y, d), z, c, g)

    def zdev(d):
        return (x, y, ring(z, d), c, g)

    def rc(src, dst, ss, rs, dev):
        return pltpu.make_async_remote_copy(
            src_ref=src, dst_ref=dst, send_sem=ss, recv_sem=rs, device_id=dev, device_id_type=MESH
        )

    ins = [
        pltpu.make_async_copy(wv_h, wraw.at[0], in_m.at[0]),
        pltpu.make_async_copy(wo_h, wraw.at[1], in_m.at[1]),
        pltpu.make_async_copy(q_h, q, in_m.at[2]),
        pltpu.make_async_copy(k_h, k, in_m.at[3]),
        pltpu.make_async_copy(hid_h, hid, in_m.at[4]),
        pltpu.make_async_copy(og_h, og, in_m.at[5]),
    ]
    for cp in ins:
        cp.start()

    barrier = pltpu.get_barrier_semaphore()
    peers = [row(i) for i in range(1, 8)] + [ydev(d) for d in (1, 2, 3)] + [zdev(d) for d in (1, 2, 3)]
    for dev in peers:
        pl.semaphore_signal(barrier, inc=1, device_id=dev, device_id_type=MESH)

    gsb[...] = jnp.zeros_like(gsb)
    ins[0].wait()
    ins[1].wait()
    lane24 = lax.broadcasted_iota(jnp.int32, (24, 128), 1)
    sq = [jnp.sum(wraw[w].astype(F32) * wraw[w].astype(F32), axis=1, keepdims=True) for w in range(2)]
    nsend[...] = jnp.where(lane24 == 0, sq[0], sq[1])
    pl.semaphore_wait(barrier, len(peers))
    for i in range(1, 8):
        rc(nsend, nrecv.at[i - 1], nm_s.at[0], nm_r.at[0], row(i)).start()
    for w in range(2):
        for j, i in enumerate((2, 4, 6)):
            rc(
                wraw.at[w, :, lanes(768 * (oc if i & 2 else c), 768)], rawr.at[w, j],
                us_s.at[w], us_r.at[w], row(i),
            ).start()

    def probs(first, last):
        def one(h, carry):
            hc = lanes(128 * h, 128)
            for r in range(4):
                n = 128 * (r + 1)
                rr = pl.ds(128 * r, 128)
                s = nt(q[rr, hc], k[pl.ds(0, n), hc]) * SCALE
                row_at = lax.broadcasted_iota(jnp.int32, (128, n), 0) + 128 * r
                col_at = lax.broadcasted_iota(jnp.int32, (128, n), 1)
                s = jnp.where(row_at >= col_at, s, -1e30)
                e = jnp.exp(s - jnp.max(s, axis=1, keepdims=True))
                Pr[h, rr, pl.ds(0, n)] = e / jnp.sum(e, axis=1, keepdims=True)
                if r < 3:
                    Pr[h, rr, pl.ds(n, 512 - n)] = jnp.zeros((128, 512 - n), F32)
            return carry

        lax.fori_loop(first, last, one, 0)

    ins[2].wait()
    ins[3].wait()
    probs(0, 1)

    rc(nrecv, nrecv, nm_s.at[0], nm_r.at[0], sib).wait()
    sq = [nsend[...]] + [nrecv[i] for i in range(7)]
    norms = [jnp.sqrt(sq[2 * i] + sq[2 * i + 1] + EPS) for i in range(4)]
    nrm[...] = norms[0]

    def unit_rows(w):
        rc(rawr.at[w], rawr.at[w], us_s.at[w], us_r.at[w], sib).wait()
        div = [norms[i][:, w : w + 1] for i in range(4)]
        unit[w] = wraw[w].astype(F32) / div[0]
        near = (unit[w, :, lanes(768 * c, 768)], rawr[w, 0].astype(F32) / div[1])
        far = (rawr[w, 1].astype(F32) / div[2], rawr[w, 2].astype(F32) / div[3])
        for i, (mine, other) in enumerate((near, far)):
            low = jnp.where(c == 0, mine, other)
            high = jnp.where(c == 0, other, mine)
            block = jnp.concatenate([low, high], axis=0)
            U48[w, i] = block
            W[w, 1 - x if i else x, y, z, :, lanes(768 * c, 768)] = block.astype(BF16)

    unit_rows(0)

    def cols(s):
        return lanes(768 * c + 384 * s, 384)

    def own_block(w, f, s):
        return W.at[w, g if f else og_, y, z, :, cols(s)]

    def plane(w, f, s, e):
        if s == 0:
            return W.at[w, g if f else og_, :, ring(z, 4 - e), :, cols(s)]
        return W.at[w, g if f else og_, ring(y, 4 - e), :, :, cols(s)]

    def ring_dev(s, first, d):
        return ydev(d) if (s == 0) == first else zdev(d)

    def first_copy(w, f, s, d):
        blk = own_block(w, f, s)
        return rc(blk, blk, p1_s.at[w, f], p1_r.at[w, f, s, d - 1], ring_dev(s, True, d))

    def second_copy(w, f, s, e, d):
        xx = g if f else og_
        if s == 0:
            blk = W.at[w, xx, ring(y, 4 - e), z, :, cols(s)]
        else:
            blk = W.at[w, xx, y, ring(z, 4 - e), :, cols(s)]
        return rc(blk, blk, p2_s.at[w, f], p2_r.at[w, f, s, d - 1], ring_dev(s, False, d))

    def sib_copy(w, f, s, e):
        blk = plane(w, f, s, e)
        return rc(blk, blk, sb_s.at[w, f], sb_r.at[w, f], sib)

    def gather_first(w, f):
        for d in (1, 3, 2):
            for s in range(2):
                first_copy(w, f, s, d).start()
        for d in (1, 3, 2):
            for s in range(2):
                second_copy(w, f, s, 0, d).start()

    def gather_second(w, f):
        for d in (1, 3, 2):
            for s in range(2):
                first_copy(w, f, s, d).wait_recv()
                for e in (1, 3, 2):
                    second_copy(w, f, s, d, e).start()
        for s in range(2):
            sib_copy(w, f, s, 0).start()

    def gather_third(w, f):
        for d in (1, 3, 2):
            for s in range(2):
                blk = plane(w, f, s, d)
                rc(blk, blk, p2_s.at[w, f], p2_r.at[w, f, s, d - 1], sib).wait_recv()
                sib_copy(w, f, s, d).start()

    def gather_last(w, f):
        blk = W.at[w, g if f else og_, :, :, :, lanes(768 * oc, 768)]
        rc(blk, blk, sb_s.at[w, f], sb_r.at[w, f], sib).wait_recv()

    def gather_sent(w, f):
        blk = W.at[w, 0, 0, 0:3, :, pl.ds(0, 768)]
        rc(blk, blk, p1_s.at[w, f], p1_r.at[w, f, 0, 0], sib).wait_send()
        blk = W.at[w, 0, 0:3, :, :, pl.ds(0, 768)]
        rc(blk, blk, p2_s.at[w, f], p2_r.at[w, f, 0, 0], sib).wait_send()
        blk = W.at[w, 0, :, :, :, pl.ds(0, 768)]
        rc(blk, blk, sb_s.at[w, f], sb_r.at[w, f], sib).wait_send()

    gather_first(0, 0)
    unit_rows(1)
    probs(1, 3)
    gather_second(0, 0)
    probs(3, 6)
    ins[4].wait()
    gather_third(0, 0)
    gather_first(0, 1)
    gather_last(0, 0)

    exs = {}

    def exchange(i, src, dst):
        exs[i] = rc(src, dst, ex_s.at[i], ex_r.at[i], mate)
        exs[i].start()

    def trows(t):
        return pl.ds(256 * t, 256)

    for t in range(2):
        vsend[t] = nt(hid[trows(t), :], W[0, og_].reshape(768, 1536)).astype(BF16)
        exchange(t, vsend.at[t], vrecv.at[t])
    gather_second(0, 1)
    gather_first(1, 0)
    gather_third(0, 1)
    gather_last(0, 1)
    for t in range(2):
        vown[t] = nt(hid[trows(t), :], W[0, g].reshape(768, 1536))
    gather_second(1, 0)
    gather_first(1, 1)
    own_heads = lanes(768 * g, 768)
    mate_heads = lanes(768 * og_, 768)
    for t in range(2):
        exs[t].wait()
        V[trows(t), :] = (vown[t] + vrecv[t].astype(F32)).astype(BF16)

        def fwd(h, carry):
            n = 256 * (t + 1)
            ATT[trows(t), lanes(768 * g + 128 * h, 128)] = nn(
                Pr[h, trows(t), pl.ds(0, n)].astype(BF16), V[pl.ds(0, n), lanes(128 * h, 128)]
            ).astype(BF16)
            return carry

        lax.fori_loop(0, 6, fwd, 0)
        blk = ATT.at[trows(t), own_heads]
        exchange(2 + t, blk, blk)
        if t == 0:
            gather_third(1, 0)
            gather_second(1, 1)
    gather_last(1, 0)
    gather_third(1, 1)
    gather_last(1, 1)

    lane = lax.broadcasted_iota(jnp.int32, (16, 128), 1)

    def row_sums(first, parts):
        acc = jnp.zeros((16, 128), F32)
        for j, v in zip(first, parts):
            acc = jnp.where(lane == j, jnp.sum(v, axis=1, keepdims=True), acc)
        return acc

    def early_sums(i, carry):
        rr = pl.ds(pl.multiple_of(16 * i, 16), 16)
        kh = (1.0 - al[...]) * hid[rr, :].astype(F32)
        mom[rr, :] = row_sums((1, 4), (kh * kh, og[rr, :].astype(F32) * kh))
        return carry

    def late_sums(i, carry):
        rr = pl.ds(pl.multiple_of(16 * i, 16), 16)
        a = al[...]
        p = proj[rr, :]
        ap = a * p
        kh = (1.0 - a) * hid[rr, :].astype(F32)
        parts = (p * p, kh * ap, ap * ap, og[rr, :].astype(F32) * ap)
        mom[rr, :] += row_sums((0, 2, 3, 5), parts)
        return carry

    def apply(i, carry):
        rr = pl.ds(pl.multiple_of(16 * i, 16), 16)
        a = al[...]
        m = mom[rr, :]
        p = proj[rr, :]
        hf = hid[rr, :].astype(F32)
        go = og[rr, :].astype(F32)
        pr, mr, gc, pc = (m[:, j : j + 1] for j in range(4))
        mixed = hf + a * (p * pr - hf)
        og[rr, :] = (mixed * mr).astype(BF16)
        gmix = mr * (go - mixed * gc)
        proj[rr, :] = gmix * (1.0 - a)
        gpb[rr, :] = (pr * (gmix * a - p * pc)).astype(BF16)
        return carry

    def proj_own(t):
        def one(n, carry):
            nc = lanes(384 * n, 384)
            proj[trows(t), nc] = nn(ATT[trows(t), own_heads], W[1, g, :, :, :, nc].reshape(768, 384))
            return carry

        lax.fori_loop(0, 4, one, 0)

    def ga_own(t):
        vown[t] = nt(gpb[trows(t), :], W[1, g].reshape(768, 1536))

    ins[5].wait()
    proj_own(0)
    lax.fori_loop(0, 32, early_sums, 0, unroll=4)
    for t in range(2):
        exs[2 + t].wait()

        def proj_more(n, carry):
            nc = lanes(384 * n, 384)
            proj[trows(t), nc] += nn(ATT[trows(t), mate_heads], W[1, og_, :, :, :, nc].reshape(768, 384))
            return carry

        lax.fori_loop(0, 4, proj_more, 0)
        lax.fori_loop(16 * t, 16 * t + 16, late_sums, 0, unroll=4)
        msend[t] = mom[trows(t), :].T[:8]
        mcp = rc(msend.at[t], mrecv.at[t], nm_s.at[1 + t], nm_r.at[1 + t], mate)
        mcp.start()
        if t == 0:
            proj_own(1)
        mcp.wait()
        m = [msend[t, pl.ds(j, 1), :] + mrecv[t, pl.ds(j, 1), :] for j in range(6)]
        pr = lax.rsqrt(m[0] / D + EPS)
        mr = lax.rsqrt((m[1] + 2.0 * pr * m[2] + pr * pr * m[3]) / D + EPS)
        gm = (m[4] + pr * m[5]) / D
        pm = (mr * m[5] - mr * mr * mr * gm * (m[2] + pr * m[3])) / D
        zero = jnp.zeros_like(pr)
        eight = jnp.concatenate([pr, mr, mr * mr * gm, pr * pr * pm, zero, zero, zero, zero], axis=0)
        mom[trows(t), :] = jnp.concatenate([eight, jnp.zeros((120, 256), F32)], axis=0).T
        lax.fori_loop(16 * t, 16 * t + 16, apply, 0, unroll=4)
        for j in range(2):
            gasend[t, j] = nt(gpb[trows(t), :], W[1, og_, 2 * j : 2 * j + 2].reshape(384, 1536)).astype(BF16)
            exchange(4 + 2 * t + j, gasend.at[t, j], garecv.at[t, j])
        ga_own(t)
    outs = [pltpu.make_async_copy(og, nh_h, out_m.at[0])]
    outs[0].start()

    gsc = {}

    def half(p):
        return g if p == 0 else og_

    def rs_partner(w, p, j, left, right):
        rr = pl.ds(384 * j, 384)
        gss[p, rr, :] = tn(
            left[:, lanes(768 * half(p) + 384 * j, 384)], right[:, lanes(768 * oc, 768)]
        ).astype(BF16)
        gsc[w, p, j] = rc(gss.at[p, rr], gsr.at[w, p, rr], gs_s.at[w, p, j], gs_r.at[w, p, j], sib)
        gsc[w, p, j].start()

    def rs_own(w, p, j, left, right):
        part = tn(left[:, lanes(768 * half(p) + 384 * j, 384)], right[:, lanes(768 * c, 768)])
        gsc[w, p, j].wait()
        total = part + gsr[w, p, pl.ds(384 * j, 384), :].astype(F32)
        RSA[w, p, 2 * j : 2 * j + 2] = total.astype(BF16).reshape(2, 4, 48, 768)

    def rs_first(w, p):
        for d in (1, 3, 2):
            rc(
                RSA.at[w, p, :, ring(z, d), :, pl.ds(0, 384)], r1b.at[w, p, 0, d - 1],
                r1_s.at[w, p], r1_r.at[w, p, 0], zdev(d),
            ).start()
            rc(
                RSA.at[w, p, ring(y, d), :, :, pl.ds(384, 384)], r1b.at[w, p, 1, d - 1],
                r1_s.at[w, p], r1_r.at[w, p, 1], ydev(d),
            ).start()

    def rs_second(w, p):
        for s in range(2):
            rc(r1b.at[w, p, s], r1b.at[w, p, s], r1_s.at[w, p], r1_r.at[w, p, s], sib).wait_recv()
            for b in range(4):
                if s == 0:
                    acc = RSA[w, p, b, z, :, pl.ds(0, 384)].astype(F32)
                else:
                    acc = RSA[w, p, y, b, :, pl.ds(384, 384)].astype(F32)
                for d in range(3):
                    acc += r1b[w, p, s, d, b].astype(F32)
                S1[w, p, s, b] = acc.astype(BF16)
            for d in (1, 3, 2):
                at = ring(y, d) if s == 0 else ring(z, d)
                rc(
                    S1.at[w, p, s, at], r2b.at[w, p, s, d - 1],
                    r2_s.at[w, p], r2_r.at[w, p, s], ring_dev(s, True, d),
                ).start()

    def rs_third(w, p):
        for s in range(2):
            rc(r2b.at[w, p, s], r2b.at[w, p, s], r2_s.at[w, p], r2_r.at[w, p, s], sib).wait_recv()
            acc = S1[w, p, s, y if s == 0 else z].astype(F32)
            for d in range(3):
                acc += r2b[w, p, s, d].astype(F32)
            xk[w, p, :, pl.ds(384 * s, 384)] = acc

    def rs_sent(w, p):
        rc(r1b.at[w, p], r1b.at[w, p], r1_s.at[w, p], r1_r.at[w, p, 0], sib).wait_send()
        rc(r2b.at[w, p], r2b.at[w, p], r2_s.at[w, p], r2_r.at[w, p, 0], sib).wait_send()

    away = jnp.where(x == g, 1, 0)
    mine = pl.ds(pl.multiple_of(24 * c, 8), 24)
    theirs = pl.ds(pl.multiple_of(24 * oc, 8), 24)

    def owner_first(w):
        far = xk[w, away]
        for i in range(2):
            xs[w, i] = far[24 * i : 24 * i + 24].astype(BF16)
        rc(xs.at[w, c], xr.at[w, 0], fd_s.at[w, 0], fd_r.at[w, 0], row(4)).start()
        rc(xs.at[w, oc], xr.at[w, 1], fd_s.at[w, 0], fd_r.at[w, 0], row(6)).start()
        near = xk.at[w, 1 - away]
        rc(near.at[theirs], gpt.at[w], fd_s.at[w, 1], fd_r.at[w, 1], sib).start()
        for i, part in enumerate((near[...], far)):
            dots = jnp.sum(part * U48[w, i], axis=1, keepdims=True)
            rds[w, i] = jnp.broadcast_to(dots, (48, 128))
        for i in range(1, 8):
            rc(
                rds.at[w, 1 if i & 4 else 0, theirs if i & 2 else mine], rdr.at[w, i - 1],
                fd_s.at[w, 2], fd_r.at[w, 2], row(i),
            ).start()

    def owner_last(w, dst, sem):
        rc(rdr.at[w], rdr.at[w], fd_s.at[w, 2], fd_r.at[w, 2], sib).wait()
        dot = rds[w, 0, mine, :]
        for i in range(7):
            dot += rdr[w, i]
        rc(gpt.at[w], gpt.at[w], fd_s.at[w, 1], fd_r.at[w, 1], sib).wait()
        rc(xr.at[w], xr.at[w], fd_s.at[w, 0], fd_r.at[w, 0], sib).wait()
        halves = (xk[w, 1 - away, mine, :] + xr[w, 0].astype(F32), gpt[w] + xr[w, 1].astype(F32))
        for at, part in zip((c, oc), halves):
            nc = lanes(768 * at, 768)
            gown[w, :, nc] = (part - unit[w, :, nc] * dot[:, :1]) / nrm[:, w : w + 1]
        cp = pltpu.make_async_copy(gown.at[w], dst, sem)
        cp.start()
        outs.append(cp)

    def bwd(h, carry):
        hc = lanes(128 * h, 128)
        for r in range(4):
            n = 128 * (r + 1)
            rr = pl.ds(128 * r, 128)
            gp = nt(GA[rr, hc], V[pl.ds(0, n), hc])
            pb = Pr[h, rr, pl.ds(0, n)]
            delta = jnp.sum(pb * gp, axis=1, keepdims=True)
            gs = (pb * (gp - delta)).astype(BF16)
            gsb[rr, pl.ds(0, n)] = gs
            gq[rr, hc] = (nn(gs, k[pl.ds(0, n), hc]) * SCALE).astype(BF16)
        gk[:, hc] = (tn(gsb[...], q[:, hc]) * SCALE).astype(BF16)
        return carry

    def value_grad(h, carry):
        hc = lanes(128 * h, 128)
        GV[:, lanes(768 * g + 128 * h, 128)] = tn(Pr[h].astype(BF16), GA[:, hc]).astype(BF16)
        return carry

    for p in range(2):
        for j in range(2):
            rs_partner(1, p, j, ATT, gpb)
    for p in range(2):
        for j in range(2):
            rs_own(1, p, j, ATT, gpb)
        rs_first(1, p)
    for j in range(2):
        exs[4 + j].wait()
        exs[6 + j].wait()
        jc = pl.ds(384 * j, 384)
        for t in range(2):
            GA[trows(t), jc] = (vown[t, :, jc] + garecv[t, j].astype(F32)).astype(BF16)
        lax.fori_loop(3 * j, 3 * j + 3, value_grad, 0)
        blk = GV.at[:, lanes(768 * g + 384 * j, 384)]
        exchange(8 + j, blk, blk)

    for j in range(2):
        rs_partner(0, 0, j, GV, hid)
    for j in range(2):
        rs_own(0, 0, j, GV, hid)
    rs_first(0, 0)
    lax.fori_loop(0, 1, bwd, 0)
    rs_second(1, 0)
    rs_second(1, 1)
    for j in range(2):
        exs[8 + j].wait()
        rs_partner(0, 1, j, GV, hid)
        rs_own(0, 1, j, GV, hid)
    rs_first(0, 1)

    def hidden_grad(n, carry):
        nc = lanes(384 * n, 384)
        gpb[:, nc] = (proj[:, nc] + nn(GV[...], W[0, :, :, :, :, nc].reshape(1536, 384))).astype(BF16)
        return carry

    rs_second(0, 0)
    rs_third(1, 0)
    rs_third(1, 1)
    owner_first(1)
    lax.fori_loop(1, 4, bwd, 0)
    rs_second(0, 1)
    owner_last(1, gwo_h, out_m.at[4])
    rs_third(0, 0)
    lax.fori_loop(4, 6, bwd, 0)
    outs.append(pltpu.make_async_copy(gq, gq_h, out_m.at[1]))
    outs.append(pltpu.make_async_copy(gk, gk_h, out_m.at[2]))
    outs[-2].start()
    outs[-1].start()
    rs_third(0, 1)
    owner_first(0)
    lax.fori_loop(0, 4, hidden_grad, 0)
    outs.append(pltpu.make_async_copy(gpb, gh_h, out_m.at[3]))
    outs[-1].start()
    owner_last(0, gwv_h, out_m.at[5])
    for w in range(2):
        for f in range(2):
            gather_sent(w, f)
            rs_sent(w, f)
    for cp in outs:
        cp.wait()


def place(*refs):
    src, dst, buf = refs[:6], refs[6:12], refs[12:18]
    sem = refs[18]
    loads = [pltpu.make_async_copy(src[i], buf[i], sem.at[0, i]) for i in range(6)]
    stores = [pltpu.make_async_copy(buf[i], dst[i], sem.at[1, i]) for i in range(6)]
    for cp in loads:
        cp.start()
    for i in range(6):
        loads[i].wait()
        stores[i].start()
    for cp in stores:
        cp.wait()


def shards(hidden, queries, attn_keys, w_value, w_out, alpha, out_grad):
    vm = pltpu.VMEM
    dma = pltpu.SemaphoreType.DMA
    hbm = pl.BlockSpec(memory_space=pltpu.HBM)
    scratch = [
        vm((512, 1536), BF16), vm((512, 768), BF16), vm((512, 768), BF16), vm((512, 1536), BF16),
        vm((2, 24, 1536), BF16), vm((2, 24, 1536), F32), vm((24, 128), F32),
        vm((24, 128), F32), vm((7, 24, 128), F32), vm((2, 3, 24, 768), BF16), vm((2, 2, 48, 768), F32),
        vm((2, 2, 4, 4, 48, 1536), BF16),
        vm((2, 256, 768), BF16), vm((2, 256, 768), BF16), vm((2, 256, 768), F32), vm((512, 768), BF16),
        vm((6, 512, 512), F32), vm((512, 1536), BF16), vm((512, 1536), F32), vm((512, 1536), BF16),
        vm((512, 128), F32), vm((2, 8, 256), F32), vm((2, 8, 256), F32),
        vm((2, 2, 256, 384), BF16), vm((2, 2, 256, 384), BF16), vm((512, 768), BF16), vm((512, 512), BF16),
        vm((512, 768), BF16), vm((512, 768), BF16), vm((512, 1536), BF16),
        vm((2, 768, 768), BF16), vm((2, 2, 768, 768), BF16), vm((2, 2, 4, 4, 48, 768), BF16),
        vm((2, 2, 2, 3, 4, 48, 384), BF16), vm((2, 2, 2, 4, 48, 384), BF16), vm((2, 2, 2, 3, 48, 384), BF16),
        vm((2, 2, 48, 768), F32), vm((2, 2, 24, 768), BF16), vm((2, 2, 24, 768), BF16),
        vm((2, 24, 768), F32), vm((2, 24, 1536), F32), vm((2, 2, 48, 128), F32), vm((2, 7, 24, 128), F32),
        dma((6,)), dma((6,)), dma((3,)), dma((3,)), dma((2,)), dma((2,)),
        dma((2, 2)), dma((2, 2, 2, 3)), dma((2, 2)), dma((2, 2, 2, 3)), dma((2, 2)), dma((2, 2)),
        dma((10,)), dma((10,)), dma((2, 2, 2)), dma((2, 2, 2)),
        dma((2, 2)), dma((2, 2, 2)), dma((2, 2)), dma((2, 2, 2)),
        dma((2, 3)), dma((2, 3)),
    ]
    sds = jax.ShapeDtypeStruct
    shapes = (
        sds((512, 1536), BF16), sds((512, 1536), BF16), sds((512, 768), BF16),
        sds((512, 768), BF16), sds((24, 1536), F32), sds((24, 1536), F32),
    )
    made = pl.pallas_call(
        kernel,
        out_shape=shapes,
        in_specs=[hbm] * 5 + [pl.BlockSpec(memory_space=pltpu.VMEM), hbm],
        out_specs=[hbm] * 6,
        scratch_shapes=scratch,
        compiler_params=pltpu.CompilerParams(
            collective_id=0, has_side_effects=True, vmem_limit_bytes=67043328
        ),
        name="sublayer",
    )(hidden, queries, attn_keys, w_value, w_out, alpha.reshape(1, 1536), out_grad)
    return pl.pallas_call(
        place,
        out_shape=shapes,
        in_specs=[hbm] * 6,
        out_specs=[hbm] * 6,
        scratch_shapes=[vm(v.shape, v.dtype) for v in shapes] + [dma((2, 6))],
        name="place",
    )(*made)


def solution(mesh):
    torus = Mesh(mesh.devices.reshape(2, 4, 4, 2, mesh.shape["grp"]), AXES)
    both = P(FSDP, "grp")
    return jax.shard_map(
        shards,
        mesh=torus,
        in_specs=(both, both, both, both, both, P("grp"), both),
        out_specs=(both,) * 6,
        check_vma=False,
    )
```

time: 177 us -> 138 us (0.78)
  Pallas kernels: 166 us -> 136 us
  local copies, waits for them, and re-layouts: 9.37 us -> 1.29 us
    pallas_call x1 -> x2, Pallas kernels: 166 us -> 136 us  [the longest x1 132 us: shards(): pl.pallas_call(kernel, out_shape=shapes, in_specs=[hbm] * 5 + [pl.BlockSp...]
    unnamed x16 -> x0, local copies, waits for them, and re-layouts: 8.07 us -> none
where the time goes in v2:
time: 138 us
  Pallas kernels  136 us (99%)
    pallas_call x1, Pallas kernels, shards(): pl.pallas_call(kernel, out_shape=shapes, in_specs=[hbm] * 5 + [pl.BlockSp...  132 us
    pallas_call x1, Pallas kernels, shards(): pl.pallas_call(place, out_shape=shapes, in_specs=[hbm] * 6, out_specs=[hb...  3.77 us

profile of v2, /device:TPU:1, one launch (start us, length us, event | category | flops | bytes accessed | tf_op | source)
XLA Modules:
  0.0 137.6 jit_solution(3387961579707443034)
XLA Ops:
  0.6 1.3 reshape.15.al
  1.9 131.7 %sublayer.1 = (bf16[512,1536]{1,0:T(8,128)(2,1)}, bf16[512,1536]{1,0:T(8,128)(2,1)}, bf16[512,768]{1,0:T(8,128)(2,1)}, bf16[512,768]{1,0:T(8,128)(2,1)}, f32[24,1536]{1,0:T(8,128)}, /*index=5*/f32[24,1536]{1,0:T(8,128)}) custom-call(bf16[512,1536]{1,0:T(8,128)(2,1)} %hid_h.1, bf16[512,768]{1,0:T(8,128)(2,1)} %q_h.1, bf16[512,768]{1,0:T(8,128)(2,1)} %k_h.1, ...), custom_call_target="tpu_custom_call" | custom-call | tf_op jit(solution)/shard_map/sublayer/pallas_call | solution.py:567
  133.7 3.8 %place.1 = (bf16[512,1536]{1,0:T(8,128)(2,1)}, bf16[512,1536]{1,0:T(8,128)(2,1)}, bf16[512,768]{1,0:T(8,128)(2,1)}, bf16[512,768]{1,0:T(8,128)(2,1)}, f32[24,1536]{1,0:T(8,128)}, /*index=5*/f32[24,1536]{1,0:T(8,128)}) custom-call(bf16[512,1536]{1,0:T(8,128)(2,1)} %get-tuple-element.12.refs_0_, bf16[512,1536]{1,0:T(8,128)(2,1)} %get-tuple-element.13.refs_1_, ...), custom_call_target="tpu_custom_call" | custom-call | tf_op jit(solution)/shard_map/place/pallas_call | solution.py:578

commit v3 on v2

--- a/solution.py
+++ b/solution.py
@@ -33,9 +33,9 @@
 
 
 def kernel(
-    hid_h, q_h, k_h, wv_h, wo_h, al, og_h,
+    hid_h, q_h, k_h, wv_h, wo_h, al_1, og_h,
     nh_h, gh_h, gq_h, gk_h, gwv_h, gwo_h,
-    hid, q, k, og, wraw, unit, nrm, nsend, nrecv, rawr, U48, W,
+    al, hid, q, k, og, wraw, unit, nrm, nsend, nrecv, rawr, U48, W,
     vsend, vrecv, vown, V, Pr, ATT, proj, gpb, mom, msend, mrecv,
     gasend, garecv, GA, gsb, gq, gk, GV, gss, gsr, RSA, r1b, S1, r2b, xk, xs, xr, gpt, gown, rds, rdr,
     in_m, out_m, nm_s, nm_r, us_s, us_r, p1_s, p1_r, p2_s, p2_r, sb_s, sb_r,
@@ -82,6 +82,7 @@
         pl.semaphore_signal(barrier, inc=1, device_id=dev, device_id_type=MESH)
 
     gsb[...] = jnp.zeros_like(gsb)
+    al[...] = al_1[...].reshape(1, 1536)
     ins[0].wait()
     ins[1].wait()
     lane24 = lax.broadcasted_iota(jnp.int32, (24, 128), 1)
@@ -173,6 +174,8 @@
         for d in (1, 3, 2):
             for s in range(2):
                 first_copy(w, f, s, d).start()
+
+    def gather_own(w, f):
         for d in (1, 3, 2):
             for s in range(2):
                 second_copy(w, f, s, 0, d).start()
@@ -206,13 +209,15 @@
         rc(blk, blk, sb_s.at[w, f], sb_r.at[w, f], sib).wait_send()
 
     gather_first(0, 0)
+    gather_own(0, 0)
     unit_rows(1)
     probs(1, 3)
     gather_second(0, 0)
     probs(3, 6)
+    gather_first(0, 1)
     ins[4].wait()
     gather_third(0, 0)
-    gather_first(0, 1)
+    gather_own(0, 1)
     gather_last(0, 0)
 
     exs = {}
@@ -229,14 +234,31 @@
         exchange(t, vsend.at[t], vrecv.at[t])
     gather_second(0, 1)
     gather_first(1, 0)
+    gather_own(1, 0)
+    gather_first(1, 1)
     gather_third(0, 1)
+    gather_second(1, 0)
+    gather_own(1, 1)
+    gather_second(1, 1)
     gather_last(0, 1)
     for t in range(2):
         vown[t] = nt(hid[trows(t), :], W[0, g].reshape(768, 1536))
-    gather_second(1, 0)
-    gather_first(1, 1)
     own_heads = lanes(768 * g, 768)
     mate_heads = lanes(768 * og_, 768)
+    lane = lax.broadcasted_iota(jnp.int32, (16, 128), 1)
+
+    def row_sums(first, parts):
+        acc = jnp.zeros((16, 128), F32)
+        for j, v in zip(first, parts):
+            acc = jnp.where(lane == j, jnp.sum(v, axis=1, keepdims=True), acc)
+        return acc
+
+    def early_sums(i, carry):
+        rr = pl.ds(pl.multiple_of(16 * i, 16), 16)
+        kh = (1.0 - al[...]) * hid[rr, :].astype(F32)
+        mom[rr, :] = row_sums((1, 4), (kh * kh, og[rr, :].astype(F32) * kh))
+        return carry
+
     for t in range(2):
         exs[t].wait()
         V[trows(t), :] = (vown[t] + vrecv[t].astype(F32)).astype(BF16)
@@ -248,29 +270,21 @@
             ).astype(BF16)
             return carry
 
-        lax.fori_loop(0, 6, fwd, 0)
-        blk = ATT.at[trows(t), own_heads]
-        exchange(2 + t, blk, blk)
         if t == 0:
-            gather_third(1, 0)
-            gather_second(1, 1)
+            lax.fori_loop(0, 6, fwd, 0)
+            blk = ATT.at[trows(0), own_heads]
+            exchange(2, blk, blk)
+            ins[5].wait()
+            lax.fori_loop(0, 32, early_sums, 0, unroll=4)
+        else:
+            lax.fori_loop(0, 3, fwd, 0)
+            blk = ATT.at[trows(1), lanes(768 * g, 384)]
+            exchange(3, blk, blk)
+            lax.fori_loop(3, 6, fwd, 0)
+    gather_third(1, 0)
+    gather_third(1, 1)
     gather_last(1, 0)
-    gather_third(1, 1)
     gather_last(1, 1)
-
-    lane = lax.broadcasted_iota(jnp.int32, (16, 128), 1)
-
-    def row_sums(first, parts):
-        acc = jnp.zeros((16, 128), F32)
-        for j, v in zip(first, parts):
-            acc = jnp.where(lane == j, jnp.sum(v, axis=1, keepdims=True), acc)
-        return acc
-
-    def early_sums(i, carry):
-        rr = pl.ds(pl.multiple_of(16 * i, 16), 16)
-        kh = (1.0 - al[...]) * hid[rr, :].astype(F32)
-        mom[rr, :] = row_sums((1, 4), (kh * kh, og[rr, :].astype(F32) * kh))
-        return carry
 
     def late_sums(i, carry):
         rr = pl.ds(pl.multiple_of(16 * i, 16), 16)
@@ -308,25 +322,23 @@
     def ga_own(t):
         vown[t] = nt(gpb[trows(t), :], W[1, g].reshape(768, 1536))
 
-    ins[5].wait()
-    proj_own(0)
-    lax.fori_loop(0, 32, early_sums, 0, unroll=4)
-    for t in range(2):
-        exs[2 + t].wait()
-
-        def proj_more(n, carry):
+    def proj_more(t):
+        def one(n, carry):
             nc = lanes(384 * n, 384)
             proj[trows(t), nc] += nn(ATT[trows(t), mate_heads], W[1, og_, :, :, :, nc].reshape(768, 384))
             return carry
 
-        lax.fori_loop(0, 4, proj_more, 0)
+        lax.fori_loop(0, 4, one, 0)
+
+    def statistics(t):
         lax.fori_loop(16 * t, 16 * t + 16, late_sums, 0, unroll=4)
         msend[t] = mom[trows(t), :].T[:8]
-        mcp = rc(msend.at[t], mrecv.at[t], nm_s.at[1 + t], nm_r.at[1 + t], mate)
-        mcp.start()
-        if t == 0:
-            proj_own(1)
-        mcp.wait()
+        cp = rc(msend.at[t], mrecv.at[t], nm_s.at[1 + t], nm_r.at[1 + t], mate)
+        cp.start()
+        return cp
+
+    def gradients(t, cp):
+        cp.wait()
         m = [msend[t, pl.ds(j, 1), :] + mrecv[t, pl.ds(j, 1), :] for j in range(6)]
         pr = lax.rsqrt(m[0] / D + EPS)
         mr = lax.rsqrt((m[1] + 2.0 * pr * m[2] + pr * pr * m[3]) / D + EPS)
@@ -336,10 +348,37 @@
         eight = jnp.concatenate([pr, mr, mr * mr * gm, pr * pr * pm, zero, zero, zero, zero], axis=0)
         mom[trows(t), :] = jnp.concatenate([eight, jnp.zeros((120, 256), F32)], axis=0).T
         lax.fori_loop(16 * t, 16 * t + 16, apply, 0, unroll=4)
-        for j in range(2):
-            gasend[t, j] = nt(gpb[trows(t), :], W[1, og_, 2 * j : 2 * j + 2].reshape(384, 1536)).astype(BF16)
-            exchange(4 + 2 * t + j, gasend.at[t, j], garecv.at[t, j])
-        ga_own(t)
+
+    def ga_part(t, j):
+        gasend[t, j] = nt(gpb[trows(t), :], W[1, og_, 2 * j : 2 * j + 2].reshape(384, 1536)).astype(BF16)
+
+    def ga_exchange(t, j):
+        exchange(5 + 2 * t + j, gasend.at[t, j], garecv.at[t, j])
+
+    proj_own(0)
+    exs[2].wait_recv()
+    proj_more(0)
+    stat0 = statistics(0)
+    blk = ATT.at[trows(1), lanes(768 * g + 384, 384)]
+    exchange(4, blk, blk)
+    proj_own(1)
+    gradients(0, stat0)
+    ga_part(0, 0)
+    ga_exchange(0, 0)
+    ga_part(0, 1)
+    exs[3].wait_recv()
+    exs[4].wait_recv()
+    proj_more(1)
+    stat1 = statistics(1)
+    ga_exchange(0, 1)
+    ga_own(0)
+    gradients(1, stat1)
+    for j in range(2):
+        ga_part(1, j)
+        ga_exchange(1, j)
+    ga_own(1)
+    for i in range(2, 5):
+        exs[i].wait_send()
     outs = [pltpu.make_async_copy(og, nh_h, out_m.at[0])]
     outs[0].start()
 
@@ -363,7 +402,7 @@
         RSA[w, p, 2 * j : 2 * j + 2] = total.astype(BF16).reshape(2, 4, 48, 768)
 
     def rs_first(w, p):
-        for d in (1, 3, 2):
+        for d in (2, 1, 3):
             rc(
                 RSA.at[w, p, :, ring(z, d), :, pl.ds(0, 384)], r1b.at[w, p, 0, d - 1],
                 r1_s.at[w, p], r1_r.at[w, p, 0], zdev(d),
@@ -384,7 +423,7 @@
                 for d in range(3):
                     acc += r1b[w, p, s, d, b].astype(F32)
                 S1[w, p, s, b] = acc.astype(BF16)
-            for d in (1, 3, 2):
+            for d in (2, 1, 3):
                 at = ring(y, d) if s == 0 else ring(z, d)
                 rc(
                     S1.at[w, p, s, at], r2b.at[w, p, s, d - 1],
@@ -409,20 +448,25 @@
 
     def owner_first(w):
         far = xk[w, away]
-        for i in range(2):
-            xs[w, i] = far[24 * i : 24 * i + 24].astype(BF16)
-        rc(xs.at[w, c], xr.at[w, 0], fd_s.at[w, 0], fd_r.at[w, 0], row(4)).start()
-        rc(xs.at[w, oc], xr.at[w, 1], fd_s.at[w, 0], fd_r.at[w, 0], row(6)).start()
-        near = xk.at[w, 1 - away]
-        rc(near.at[theirs], gpt.at[w], fd_s.at[w, 1], fd_r.at[w, 1], sib).start()
-        for i, part in enumerate((near[...], far)):
+        near = xk[w, 1 - away]
+        for i, part in enumerate((near, far)):
             dots = jnp.sum(part * U48[w, i], axis=1, keepdims=True)
             rds[w, i] = jnp.broadcast_to(dots, (48, 128))
-        for i in range(1, 8):
+            xs[w, i] = far[24 * i : 24 * i + 24].astype(BF16)
+
+        def send_dots(i):
             rc(
                 rds.at[w, 1 if i & 4 else 0, theirs if i & 2 else mine], rdr.at[w, i - 1],
                 fd_s.at[w, 2], fd_r.at[w, 2], row(i),
             ).start()
+
+        for i in (1, 3, 5, 7):
+            send_dots(i)
+        rc(xs.at[w, c], xr.at[w, 0], fd_s.at[w, 0], fd_r.at[w, 0], row(4)).start()
+        rc(xs.at[w, oc], xr.at[w, 1], fd_s.at[w, 0], fd_r.at[w, 0], row(6)).start()
+        rc(xk.at[w, 1 - away, theirs], gpt.at[w], fd_s.at[w, 1], fd_r.at[w, 1], sib).start()
+        for i in (2, 4, 6):
+            send_dots(i)
 
     def owner_last(w, dst, sem):
         rc(rdr.at[w], rdr.at[w], fd_s.at[w, 2], fd_r.at[w, 2], sib).wait()
@@ -466,27 +510,31 @@
             rs_own(1, p, j, ATT, gpb)
         rs_first(1, p)
     for j in range(2):
-        exs[4 + j].wait()
-        exs[6 + j].wait()
+        exs[5 + j].wait()
+        exs[7 + j].wait()
         jc = pl.ds(384 * j, 384)
         for t in range(2):
             GA[trows(t), jc] = (vown[t, :, jc] + garecv[t, j].astype(F32)).astype(BF16)
         lax.fori_loop(3 * j, 3 * j + 3, value_grad, 0)
         blk = GV.at[:, lanes(768 * g + 384 * j, 384)]
-        exchange(8 + j, blk, blk)
+        exchange(9 + j, blk, blk)
 
     for j in range(2):
         rs_partner(0, 0, j, GV, hid)
     for j in range(2):
         rs_own(0, 0, j, GV, hid)
     rs_first(0, 0)
-    lax.fori_loop(0, 1, bwd, 0)
+    lax.fori_loop(0, 2, bwd, 0)
     rs_second(1, 0)
+    exs[9].wait()
+    rs_partner(0, 1, 0, GV, hid)
+    rs_own(0, 1, 0, GV, hid)
+    lax.fori_loop(2, 4, bwd, 0)
     rs_second(1, 1)
-    for j in range(2):
-        exs[8 + j].wait()
-        rs_partner(0, 1, j, GV, hid)
-        rs_own(0, 1, j, GV, hid)
+    rs_second(0, 0)
+    exs[10].wait()
+    rs_partner(0, 1, 1, GV, hid)
+    rs_own(0, 1, 1, GV, hid)
     rs_first(0, 1)
 
     def hidden_grad(n, carry):
@@ -494,24 +542,22 @@
         gpb[:, nc] = (proj[:, nc] + nn(GV[...], W[0, :, :, :, :, nc].reshape(1536, 384))).astype(BF16)
         return carry
 
-    rs_second(0, 0)
     rs_third(1, 0)
     rs_third(1, 1)
     owner_first(1)
-    lax.fori_loop(1, 4, bwd, 0)
-    rs_second(0, 1)
-    owner_last(1, gwo_h, out_m.at[4])
     rs_third(0, 0)
+    lax.fori_loop(0, 4, hidden_grad, 0)
+    outs.append(pltpu.make_async_copy(gpb, gh_h, out_m.at[3]))
+    outs[-1].start()
     lax.fori_loop(4, 6, bwd, 0)
     outs.append(pltpu.make_async_copy(gq, gq_h, out_m.at[1]))
     outs.append(pltpu.make_async_copy(gk, gk_h, out_m.at[2]))
     outs[-2].start()
     outs[-1].start()
+    rs_second(0, 1)
+    owner_last(1, gwo_h, out_m.at[4])
     rs_third(0, 1)
     owner_first(0)
-    lax.fori_loop(0, 4, hidden_grad, 0)
-    outs.append(pltpu.make_async_copy(gpb, gh_h, out_m.at[3]))
-    outs[-1].start()
     owner_last(0, gwv_h, out_m.at[5])
     for w in range(2):
         for f in range(2):
@@ -540,7 +586,7 @@
     dma = pltpu.SemaphoreType.DMA
     hbm = pl.BlockSpec(memory_space=pltpu.HBM)
     scratch = [
-        vm((512, 1536), BF16), vm((512, 768), BF16), vm((512, 768), BF16), vm((512, 1536), BF16),
+        vm((1, 1536), F32), vm((512, 1536), BF16), vm((512, 768), BF16), vm((512, 768), BF16), vm((512, 1536), BF16),
         vm((2, 24, 1536), BF16), vm((2, 24, 1536), F32), vm((24, 128), F32),
         vm((24, 128), F32), vm((7, 24, 128), F32), vm((2, 3, 24, 768), BF16), vm((2, 2, 48, 768), F32),
         vm((2, 2, 4, 4, 48, 1536), BF16),
@@ -555,7 +601,7 @@
         vm((2, 24, 768), F32), vm((2, 24, 1536), F32), vm((2, 2, 48, 128), F32), vm((2, 7, 24, 128), F32),
         dma((6,)), dma((6,)), dma((3,)), dma((3,)), dma((2,)), dma((2,)),
         dma((2, 2)), dma((2, 2, 2, 3)), dma((2, 2)), dma((2, 2, 2, 3)), dma((2, 2)), dma((2, 2)),
-        dma((10,)), dma((10,)), dma((2, 2, 2)), dma((2, 2, 2)),
+        dma((11,)), dma((11,)), dma((2, 2, 2)), dma((2, 2, 2)),
         dma((2, 2)), dma((2, 2, 2)), dma((2, 2)), dma((2, 2, 2)),
         dma((2, 3)), dma((2, 3)),
     ]
@@ -574,7 +620,7 @@
             collective_id=0, has_side_effects=True, vmem_limit_bytes=67043328
         ),
         name="sublayer",
-    )(hidden, queries, attn_keys, w_value, w_out, alpha.reshape(1, 1536), out_grad)
+    )(hidden, queries, attn_keys, w_value, w_out, alpha, out_grad)
     return pl.pallas_call(
         place,
         out_shape=shapes,

time: 138 us -> 128 us (0.928)
  Pallas kernels: 136 us -> 128 us
    pallas_call x1, Pallas kernels: 132 us -> 124 us  [shards(): pl.pallas_call(kernel, out_shape=shapes, in_specs=[hbm] * 5 + [pl.BlockSp...]
where the time goes in v3:
time: 128 us
  Pallas kernels  128 us (100%)
    pallas_call x1, Pallas kernels, shards(): pl.pallas_call(kernel, out_shape=shapes, in_specs=[hbm] * 5 + [pl.BlockSp...  124 us
    pallas_call x1, Pallas kernels, shards(): pl.pallas_call(place, out_shape=shapes, in_specs=[hbm] * 6, out_specs=[hb...  3.77 us

profile of v3, /device:TPU:1, one launch (start us, length us, event | category | flops | bytes accessed | tf_op | source)
XLA Modules:
  0.0 128.4 jit_solution(11840366393395459708)
XLA Ops:
  0.6 123.8 %sublayer.1 = (bf16[512,1536]{1,0:T(8,128)(2,1)}, bf16[512,1536]{1,0:T(8,128)(2,1)}, bf16[512,768]{1,0:T(8,128)(2,1)}, bf16[512,768]{1,0:T(8,128)(2,1)}, f32[24,1536]{1,0:T(8,128)}, /*index=5*/f32[24,1536]{1,0:T(8,128)}) custom-call(bf16[512,1536]{1,0:T(8,128)(2,1)} %hid_h.1, bf16[512,768]{1,0:T(8,128)(2,1)} %q_h.1, bf16[512,768]{1,0:T(8,128)(2,1)} %k_h.1, ...), custom_call_target="tpu_custom_call" | custom-call | tf_op jit(solution)/shard_map/sublayer/pallas_call | solution.py:613
  124.4 3.8 %place.1 = (bf16[512,1536]{1,0:T(8,128)(2,1)}, bf16[512,1536]{1,0:T(8,128)(2,1)}, bf16[512,768]{1,0:T(8,128)(2,1)}, bf16[512,768]{1,0:T(8,128)(2,1)}, f32[24,1536]{1,0:T(8,128)}, /*index=5*/f32[24,1536]{1,0:T(8,128)}) custom-call(bf16[512,1536]{1,0:T(8,128)(2,1)} %get-tuple-element.12.refs_0_, bf16[512,1536]{1,0:T(8,128)(2,1)} %get-tuple-element.13.refs_1_, ...), custom_call_target="tpu_custom_call" | custom-call | tf_op jit(solution)/shard_map/place/pallas_call | solution.py:624

commit v4 on v3

--- a/solution.py
+++ b/solution.py
@@ -218,8 +218,6 @@
     ins[4].wait()
     gather_third(0, 0)
     gather_own(0, 1)
-    gather_last(0, 0)
-
     exs = {}
 
     def exchange(i, src, dst):
@@ -227,22 +225,31 @@
         exs[i].start()
 
     def trows(t):
-        return pl.ds(256 * t, 256)
+        return pl.ds(128 * t, 128)
+
+    def value_part(rows, f, at):
+        nc = lanes(768 * at, 768)
+        return nt(hid[rows, nc], W[0, g if f else og_, :, :, :, nc].reshape(768, 768))
 
     for t in range(2):
-        vsend[t] = nt(hid[trows(t), :], W[0, og_].reshape(768, 1536)).astype(BF16)
+        rr = pl.ds(256 * t, 256)
+        vown[rr, :] = value_part(rr, 0, c)
+    gather_second(0, 1)
+    gather_first(1, 1)
+    gather_first(1, 0)
+    gather_last(0, 0)
+    for t in range(4):
+        vsend[t] = (vown[trows(t), :] + value_part(trows(t), 0, oc)).astype(BF16)
         exchange(t, vsend.at[t], vrecv.at[t])
-    gather_second(0, 1)
-    gather_first(1, 0)
-    gather_own(1, 0)
-    gather_first(1, 1)
     gather_third(0, 1)
-    gather_second(1, 0)
     gather_own(1, 1)
     gather_second(1, 1)
+    gather_own(1, 0)
+    gather_second(1, 0)
     gather_last(0, 1)
     for t in range(2):
-        vown[t] = nt(hid[trows(t), :], W[0, g].reshape(768, 1536))
+        rr = pl.ds(256 * t, 256)
+        vown[rr, :] = nt(hid[rr, :], W[0, g].reshape(768, 1536))
     own_heads = lanes(768 * g, 768)
     mate_heads = lanes(768 * og_, 768)
     lane = lax.broadcasted_iota(jnp.int32, (16, 128), 1)
@@ -259,31 +266,32 @@
         mom[rr, :] = row_sums((1, 4), (kh * kh, og[rr, :].astype(F32) * kh))
         return carry
 
-    for t in range(2):
-        exs[t].wait()
-        V[trows(t), :] = (vown[t] + vrecv[t].astype(F32)).astype(BF16)
-
-        def fwd(h, carry):
-            n = 256 * (t + 1)
+    def fwd(t):
+        n = 128 * (t + 1)
+
+        def one(h, carry):
             ATT[trows(t), lanes(768 * g + 128 * h, 128)] = nn(
                 Pr[h, trows(t), pl.ds(0, n)].astype(BF16), V[pl.ds(0, n), lanes(128 * h, 128)]
             ).astype(BF16)
             return carry
 
+        lax.fori_loop(0, 6, one, 0)
+
+    def attn_exchange(t):
+        blk = ATT.at[trows(t), own_heads]
+        exchange(4 + t, blk, blk)
+
+    for t in range(4):
+        exs[t].wait()
+        V[trows(t), :] = (vown[trows(t), :] + vrecv[t].astype(F32)).astype(BF16)
+        fwd(t)
+        if t < 2:
+            attn_exchange(t)
         if t == 0:
-            lax.fori_loop(0, 6, fwd, 0)
-            blk = ATT.at[trows(0), own_heads]
-            exchange(2, blk, blk)
             ins[5].wait()
             lax.fori_loop(0, 32, early_sums, 0, unroll=4)
-        else:
-            lax.fori_loop(0, 3, fwd, 0)
-            blk = ATT.at[trows(1), lanes(768 * g, 384)]
-            exchange(3, blk, blk)
-            lax.fori_loop(3, 6, fwd, 0)
-    gather_third(1, 0)
-    gather_third(1, 1)
-    gather_last(1, 0)
+        if t == 2:
+            gather_third(1, 1)
     gather_last(1, 1)
 
     def late_sums(i, carry):
@@ -311,34 +319,28 @@
         gpb[rr, :] = (pr * (gmix * a - p * pc)).astype(BF16)
         return carry
 
-    def proj_own(t):
-        def one(n, carry):
-            nc = lanes(384 * n, 384)
-            proj[trows(t), nc] = nn(ATT[trows(t), own_heads], W[1, g, :, :, :, nc].reshape(768, 384))
-            return carry
-
-        lax.fori_loop(0, 4, one, 0)
-
-    def ga_own(t):
-        vown[t] = nt(gpb[trows(t), :], W[1, g].reshape(768, 1536))
+    def proj_own(n, carry):
+        nc = lanes(384 * n, 384)
+        proj[:, nc] = nn(ATT[:, own_heads], W[1, g, :, :, :, nc].reshape(768, 384))
+        return carry
 
     def proj_more(t):
         def one(n, carry):
-            nc = lanes(384 * n, 384)
-            proj[trows(t), nc] += nn(ATT[trows(t), mate_heads], W[1, og_, :, :, :, nc].reshape(768, 384))
+            nc = lanes(768 * n, 768)
+            proj[trows(t), nc] += nn(ATT[trows(t), mate_heads], W[1, og_, :, :, :, nc].reshape(768, 768))
             return carry
 
-        lax.fori_loop(0, 4, one, 0)
+        lax.fori_loop(0, 2, one, 0)
 
     def statistics(t):
-        lax.fori_loop(16 * t, 16 * t + 16, late_sums, 0, unroll=4)
+        exs[4 + t].wait_recv()
+        proj_more(t)
+        lax.fori_loop(8 * t, 8 * t + 8, late_sums, 0, unroll=4)
         msend[t] = mom[trows(t), :].T[:8]
-        cp = rc(msend.at[t], mrecv.at[t], nm_s.at[1 + t], nm_r.at[1 + t], mate)
-        cp.start()
-        return cp
-
-    def gradients(t, cp):
-        cp.wait()
+        rc(msend.at[t], mrecv.at[t], nm_s.at[1 + t], nm_r.at[1 + t], mate).start()
+
+    def gradients(t):
+        rc(msend.at[t], mrecv.at[t], nm_s.at[1 + t], nm_r.at[1 + t], mate).wait()
         m = [msend[t, pl.ds(j, 1), :] + mrecv[t, pl.ds(j, 1), :] for j in range(6)]
         pr = lax.rsqrt(m[0] / D + EPS)
         mr = lax.rsqrt((m[1] + 2.0 * pr * m[2] + pr * pr * m[3]) / D + EPS)
@@ -346,39 +348,42 @@
         pm = (mr * m[5] - mr * mr * mr * gm * (m[2] + pr * m[3])) / D
         zero = jnp.zeros_like(pr)
         eight = jnp.concatenate([pr, mr, mr * mr * gm, pr * pr * pm, zero, zero, zero, zero], axis=0)
-        mom[trows(t), :] = jnp.concatenate([eight, jnp.zeros((120, 256), F32)], axis=0).T
-        lax.fori_loop(16 * t, 16 * t + 16, apply, 0, unroll=4)
-
-    def ga_part(t, j):
-        gasend[t, j] = nt(gpb[trows(t), :], W[1, og_, 2 * j : 2 * j + 2].reshape(384, 1536)).astype(BF16)
+        mom[trows(t), :] = jnp.concatenate([eight, jnp.zeros((120, 128), F32)], axis=0).T
+        lax.fori_loop(8 * t, 8 * t + 8, apply, 0, unroll=4)
+        part = nt(gpb[trows(t), :], W[1, og_].reshape(768, 1536)).astype(BF16)
+        gasend[t, 0] = part[:, :384]
+        gasend[t, 1] = part[:, 384:]
 
     def ga_exchange(t, j):
-        exchange(5 + 2 * t + j, gasend.at[t, j], garecv.at[t, j])
-
-    proj_own(0)
-    exs[2].wait_recv()
-    proj_more(0)
-    stat0 = statistics(0)
-    blk = ATT.at[trows(1), lanes(768 * g + 384, 384)]
-    exchange(4, blk, blk)
-    proj_own(1)
-    gradients(0, stat0)
-    ga_part(0, 0)
+        exchange(8 + 2 * t + j, gasend.at[t, j], garecv.at[t, j])
+
+    lax.fori_loop(0, 4, proj_own, 0)
+    gather_third(1, 0)
+    gather_last(1, 0)
+    statistics(0)
+    attn_exchange(2)
+    statistics(1)
+    attn_exchange(3)
+    gradients(0)
+    statistics(2)
     ga_exchange(0, 0)
-    ga_part(0, 1)
-    exs[3].wait_recv()
-    exs[4].wait_recv()
-    proj_more(1)
-    stat1 = statistics(1)
     ga_exchange(0, 1)
-    ga_own(0)
-    gradients(1, stat1)
-    for j in range(2):
-        ga_part(1, j)
-        ga_exchange(1, j)
-    ga_own(1)
-    for i in range(2, 5):
-        exs[i].wait_send()
+    gradients(1)
+    statistics(3)
+    ga_exchange(1, 0)
+    gradients(2)
+    ga_exchange(2, 0)
+    ga_exchange(1, 1)
+    rr = pl.ds(0, 256)
+    vown[rr, :] = nt(gpb[rr, :], W[1, g].reshape(768, 1536))
+    gradients(3)
+    ga_exchange(3, 0)
+    ga_exchange(2, 1)
+    ga_exchange(3, 1)
+    rr = pl.ds(256, 256)
+    vown[rr, :] = nt(gpb[rr, :], W[1, g].reshape(768, 1536))
+    for t in range(4):
+        exs[4 + t].wait_send()
     outs = [pltpu.make_async_copy(og, nh_h, out_m.at[0])]
     outs[0].start()
 
@@ -387,19 +392,25 @@
     def half(p):
         return g if p == 0 else og_
 
-    def rs_partner(w, p, j, left, right):
-        rr = pl.ds(384 * j, 384)
+    def rs_partner(w, p, lo, hi, left, right):
+        rr = pl.ds(lo, hi - lo)
         gss[p, rr, :] = tn(
-            left[:, lanes(768 * half(p) + 384 * j, 384)], right[:, lanes(768 * oc, 768)]
+            left[:, lanes(768 * half(p) + lo, hi - lo)], right[:, lanes(768 * oc, 768)]
         ).astype(BF16)
-        gsc[w, p, j] = rc(gss.at[p, rr], gsr.at[w, p, rr], gs_s.at[w, p, j], gs_r.at[w, p, j], sib)
-        gsc[w, p, j].start()
-
-    def rs_own(w, p, j, left, right):
-        part = tn(left[:, lanes(768 * half(p) + 384 * j, 384)], right[:, lanes(768 * c, 768)])
-        gsc[w, p, j].wait()
-        total = part + gsr[w, p, pl.ds(384 * j, 384), :].astype(F32)
-        RSA[w, p, 2 * j : 2 * j + 2] = total.astype(BF16).reshape(2, 4, 48, 768)
+        i = {0: 0, 384: 1, 640: 2}[lo]
+        gsc[w, p, lo] = rc(gss.at[p, rr], gsr.at[w, p, rr], gs_s.at[w, p, i], gs_r.at[w, p, i], sib)
+        gsc[w, p, lo].start()
+
+    def rs_own(w, p, lo, hi, left, right):
+        part = tn(left[:, lanes(768 * half(p) + lo, hi - lo)], right[:, lanes(768 * c, 768)])
+        gsc[w, p, lo].wait()
+        total = (part + gsr[w, p, pl.ds(lo, hi - lo), :].astype(F32)).astype(BF16)
+        at = lo
+        while at < hi:
+            n = min(48 - at % 48, hi - at)
+            b = at // 48
+            RSA[w, p, b // 4, b % 4, pl.ds(at % 48, n), :] = total[at - lo : at - lo + n]
+            at += n
 
     def rs_first(w, p):
         for d in (2, 1, 3):
@@ -502,39 +513,40 @@
         GV[:, lanes(768 * g + 128 * h, 128)] = tn(Pr[h].astype(BF16), GA[:, hc]).astype(BF16)
         return carry
 
-    for p in range(2):
-        for j in range(2):
-            rs_partner(1, p, j, ATT, gpb)
-    for p in range(2):
-        for j in range(2):
-            rs_own(1, p, j, ATT, gpb)
-        rs_first(1, p)
     for j in range(2):
-        exs[5 + j].wait()
-        exs[7 + j].wait()
+        for lo in (0, 384):
+            rs_partner(1, j, lo, lo + 384, ATT, gpb)
+        for lo in (0, 384):
+            rs_own(1, j, lo, lo + 384, ATT, gpb)
+        rs_first(1, j)
+        for t in range(4):
+            exs[8 + 2 * t + j].wait()
         jc = pl.ds(384 * j, 384)
-        for t in range(2):
-            GA[trows(t), jc] = (vown[t, :, jc] + garecv[t, j].astype(F32)).astype(BF16)
-        lax.fori_loop(3 * j, 3 * j + 3, value_grad, 0)
-        blk = GV.at[:, lanes(768 * g + 384 * j, 384)]
-        exchange(9 + j, blk, blk)
-
-    for j in range(2):
-        rs_partner(0, 0, j, GV, hid)
-    for j in range(2):
-        rs_own(0, 0, j, GV, hid)
+        for t in range(4):
+            GA[trows(t), jc] = (vown[trows(t), jc] + garecv[t, j].astype(F32)).astype(BF16)
+        lax.fori_loop(3 * j, 2 * j + 3, value_grad, 0)
+        blk = GV.at[:, lanes(768 * g + 384 * j, 384 - 128 * j)]
+        exchange(16 + j, blk, blk)
+    value_grad(5, 0)
+    blk = GV.at[:, lanes(768 * g + 640, 128)]
+    exchange(18, blk, blk)
+
+    for lo in (0, 384):
+        rs_partner(0, 0, lo, lo + 384, GV, hid)
+    for lo in (0, 384):
+        rs_own(0, 0, lo, lo + 384, GV, hid)
     rs_first(0, 0)
     lax.fori_loop(0, 2, bwd, 0)
     rs_second(1, 0)
-    exs[9].wait()
-    rs_partner(0, 1, 0, GV, hid)
-    rs_own(0, 1, 0, GV, hid)
-    lax.fori_loop(2, 4, bwd, 0)
-    rs_second(1, 1)
-    rs_second(0, 0)
-    exs[10].wait()
-    rs_partner(0, 1, 1, GV, hid)
-    rs_own(0, 1, 1, GV, hid)
+    exs[16].wait()
+    rs_partner(0, 1, 0, 384, GV, hid)
+    rs_own(0, 1, 0, 384, GV, hid)
+    exs[17].wait()
+    rs_partner(0, 1, 384, 640, GV, hid)
+    rs_own(0, 1, 384, 640, GV, hid)
+    exs[18].wait()
+    rs_partner(0, 1, 640, 768, GV, hid)
+    rs_own(0, 1, 640, 768, GV, hid)
     rs_first(0, 1)
 
     def hidden_grad(n, carry):
@@ -542,22 +554,25 @@
         gpb[:, nc] = (proj[:, nc] + nn(GV[...], W[0, :, :, :, :, nc].reshape(1536, 384))).astype(BF16)
         return carry
 
+    lax.fori_loop(0, 4, hidden_grad, 0)
+    outs.append(pltpu.make_async_copy(gpb, gh_h, out_m.at[3]))
+    outs[-1].start()
+    rs_second(1, 1)
+    rs_second(0, 0)
     rs_third(1, 0)
+    lax.fori_loop(2, 5, bwd, 0)
+    rs_second(0, 1)
     rs_third(1, 1)
     owner_first(1)
     rs_third(0, 0)
-    lax.fori_loop(0, 4, hidden_grad, 0)
-    outs.append(pltpu.make_async_copy(gpb, gh_h, out_m.at[3]))
-    outs[-1].start()
-    lax.fori_loop(4, 6, bwd, 0)
+    lax.fori_loop(5, 6, bwd, 0)
     outs.append(pltpu.make_async_copy(gq, gq_h, out_m.at[1]))
     outs.append(pltpu.make_async_copy(gk, gk_h, out_m.at[2]))
     outs[-2].start()
     outs[-1].start()
-    rs_second(0, 1)
-    owner_last(1, gwo_h, out_m.at[4])
     rs_third(0, 1)
     owner_first(0)
+    owner_last(1, gwo_h, out_m.at[4])
     owner_last(0, gwv_h, out_m.at[5])
     for w in range(2):
         for f in range(2):
@@ -590,18 +605,18 @@
         vm((2, 24, 1536), BF16), vm((2, 24, 1536), F32), vm((24, 128), F32),
         vm((24, 128), F32), vm((7, 24, 128), F32), vm((2, 3, 24, 768), BF16), vm((2, 2, 48, 768), F32),
         vm((2, 2, 4, 4, 48, 1536), BF16),
-        vm((2, 256, 768), BF16), vm((2, 256, 768), BF16), vm((2, 256, 768), F32), vm((512, 768), BF16),
+        vm((4, 128, 768), BF16), vm((4, 128, 768), BF16), vm((512, 768), F32), vm((512, 768), BF16),
         vm((6, 512, 512), F32), vm((512, 1536), BF16), vm((512, 1536), F32), vm((512, 1536), BF16),
-        vm((512, 128), F32), vm((2, 8, 256), F32), vm((2, 8, 256), F32),
-        vm((2, 2, 256, 384), BF16), vm((2, 2, 256, 384), BF16), vm((512, 768), BF16), vm((512, 512), BF16),
+        vm((512, 128), F32), vm((4, 8, 128), F32), vm((4, 8, 128), F32),
+        vm((4, 2, 128, 384), BF16), vm((4, 2, 128, 384), BF16), vm((512, 768), BF16), vm((512, 512), BF16),
         vm((512, 768), BF16), vm((512, 768), BF16), vm((512, 1536), BF16),
         vm((2, 768, 768), BF16), vm((2, 2, 768, 768), BF16), vm((2, 2, 4, 4, 48, 768), BF16),
         vm((2, 2, 2, 3, 4, 48, 384), BF16), vm((2, 2, 2, 4, 48, 384), BF16), vm((2, 2, 2, 3, 48, 384), BF16),
         vm((2, 2, 48, 768), F32), vm((2, 2, 24, 768), BF16), vm((2, 2, 24, 768), BF16),
         vm((2, 24, 768), F32), vm((2, 24, 1536), F32), vm((2, 2, 48, 128), F32), vm((2, 7, 24, 128), F32),
-        dma((6,)), dma((6,)), dma((3,)), dma((3,)), dma((2,)), dma((2,)),
+        dma((6,)), dma((6,)), dma((5,)), dma((5,)), dma((2,)), dma((2,)),
         dma((2, 2)), dma((2, 2, 2, 3)), dma((2, 2)), dma((2, 2, 2, 3)), dma((2, 2)), dma((2, 2)),
-        dma((11,)), dma((11,)), dma((2, 2, 2)), dma((2, 2, 2)),
+        dma((19,)), dma((19,)), dma((2, 2, 3)), dma((2, 2, 3)),
         dma((2, 2)), dma((2, 2, 2)), dma((2, 2)), dma((2, 2, 2)),
         dma((2, 3)), dma((2, 3)),
     ]

time: 128 us -> 126 us (0.984)
  Pallas kernels: 128 us -> 125 us
    pallas_call x1, Pallas kernels: 124 us -> 121 us  [shards(): pl.pallas_call(kernel, out_shape=shapes, in_specs=[hbm] * 5 + [pl.BlockSp...]
where the time goes in v4:
time: 126 us
  Pallas kernels  125 us (99%)
    pallas_call x1, Pallas kernels, shards(): pl.pallas_call(kernel, out_shape=shapes, in_specs=[hbm] * 5 + [pl.BlockSp...  121 us
    pallas_call x1, Pallas kernels, shards(): pl.pallas_call(place, out_shape=shapes, in_specs=[hbm] * 6, out_specs=[hb...  3.77 us

profile of v4, /device:TPU:1, one launch (start us, length us, event | category | flops | bytes accessed | tf_op | source)
XLA Modules:
  0.0 125.5 jit_solution(3544279989490146818)
XLA Ops:
  0.6 121.0 %sublayer.1 = (bf16[512,1536]{1,0:T(8,128)(2,1)}, bf16[512,1536]{1,0:T(8,128)(2,1)}, bf16[512,768]{1,0:T(8,128)(2,1)}, bf16[512,768]{1,0:T(8,128)(2,1)}, f32[24,1536]{1,0:T(8,128)}, /*index=5*/f32[24,1536]{1,0:T(8,128)}) custom-call(bf16[512,1536]{1,0:T(8,128)(2,1)} %hid_h.1, bf16[512,768]{1,0:T(8,128)(2,1)} %q_h.1, bf16[512,768]{1,0:T(8,128)(2,1)} %k_h.1, ...), custom_call_target="tpu_custom_call" | custom-call | tf_op jit(solution)/shard_map/sublayer/pallas_call | solution.py:628
  121.6 3.8 %place.1 = (bf16[512,1536]{1,0:T(8,128)(2,1)}, bf16[512,1536]{1,0:T(8,128)(2,1)}, bf16[512,768]{1,0:T(8,128)(2,1)}, bf16[512,768]{1,0:T(8,128)(2,1)}, f32[24,1536]{1,0:T(8,128)}, /*index=5*/f32[24,1536]{1,0:T(8,128)}) custom-call(bf16[512,1536]{1,0:T(8,128)(2,1)} %get-tuple-element.12.refs_0_, bf16[512,1536]{1,0:T(8,128)(2,1)} %get-tuple-element.13.refs_1_, ...), custom_call_target="tpu_custom_call" | custom-call | tf_op jit(solution)/shard_map/place/pallas_call | solution.py:639

commit v5 on v4

--- a/solution.py
+++ b/solution.py
@@ -87,7 +87,8 @@
     ins[1].wait()
     lane24 = lax.broadcasted_iota(jnp.int32, (24, 128), 1)
     sq = [jnp.sum(wraw[w].astype(F32) * wraw[w].astype(F32), axis=1, keepdims=True) for w in range(2)]
-    nsend[...] = jnp.where(lane24 == 0, sq[0], sq[1])
+    sums = jnp.where(lane24 == 0, sq[0], sq[1])
+    nsend[...] = jnp.concatenate([sums, jnp.zeros((104, 128), F32)], axis=0).T[:8]
     pl.semaphore_wait(barrier, len(peers))
     for i in range(1, 8):
         rc(nsend, nrecv.at[i - 1], nm_s.at[0], nm_r.at[0], row(i)).start()
@@ -123,11 +124,12 @@
     rc(nrecv, nrecv, nm_s.at[0], nm_r.at[0], sib).wait()
     sq = [nsend[...]] + [nrecv[i] for i in range(7)]
     norms = [jnp.sqrt(sq[2 * i] + sq[2 * i + 1] + EPS) for i in range(4)]
-    nrm[...] = norms[0]
+    norms = jnp.concatenate(norms + [jnp.zeros((96, 128), F32)], axis=0).T[:24]
+    nrm[...] = norms
 
     def unit_rows(w):
         rc(rawr.at[w], rawr.at[w], us_s.at[w], us_r.at[w], sib).wait()
-        div = [norms[i][:, w : w + 1] for i in range(4)]
+        div = [norms[:, 8 * i + w : 8 * i + w + 1] for i in range(4)]
         unit[w] = wraw[w].astype(F32) / div[0]
         near = (unit[w, :, lanes(768 * c, 768)], rawr[w, 0].astype(F32) / div[1])
         far = (rawr[w, 1].astype(F32) / div[2], rawr[w, 2].astype(F32) / div[3])
@@ -166,6 +168,17 @@
             blk = W.at[w, xx, y, ring(z, 4 - e), :, cols(s)]
         return rc(blk, blk, p2_s.at[w, f], p2_r.at[w, f, s, d - 1], ring_dev(s, False, d))
 
+    def relay_copy(w, f, s, e, d):
+        xx = g if f else og_
+        if s == 0:
+            blk = W.at[w, xx, ring(y, 4 - e), ring(z, 4 - d), :, cols(s)]
+        else:
+            blk = W.at[w, xx, ring(y, 4 - d), ring(z, 4 - e), :, cols(s)]
+        return rc(blk, blk, p2_s.at[w, f], p2_r.at[w, f, s, 1], ring_dev(s, False, d))
+
+    def steps(w):
+        return (1, 3) if w else (1, 3, 2)
+
     def sib_copy(w, f, s, e):
         blk = plane(w, f, s, e)
         return rc(blk, blk, sb_s.at[w, f], sb_r.at[w, f], sib)
@@ -176,7 +189,7 @@
                 first_copy(w, f, s, d).start()
 
     def gather_own(w, f):
-        for d in (1, 3, 2):
+        for d in steps(w):
             for s in range(2):
                 second_copy(w, f, s, 0, d).start()
 
@@ -184,16 +197,19 @@
         for d in (1, 3, 2):
             for s in range(2):
                 first_copy(w, f, s, d).wait_recv()
-                for e in (1, 3, 2):
+                for e in steps(w):
                     second_copy(w, f, s, d, e).start()
         for s in range(2):
             sib_copy(w, f, s, 0).start()
 
-    def gather_third(w, f):
-        for d in (1, 3, 2):
+    def gather_third(w, f, dirs=(1, 3, 2)):
+        for d in dirs:
             for s in range(2):
                 blk = plane(w, f, s, d)
                 rc(blk, blk, p2_s.at[w, f], p2_r.at[w, f, s, d - 1], sib).wait_recv()
+                if w and d != 2:
+                    for e in (0, 1) if d == 1 else (2, 3):
+                        relay_copy(w, f, s, e, d).start()
                 sib_copy(w, f, s, d).start()
 
     def gather_last(w, f):
@@ -290,8 +306,11 @@
         if t == 0:
             ins[5].wait()
             lax.fori_loop(0, 32, early_sums, 0, unroll=4)
+        if t == 1:
+            gather_third(1, 1, (1, 3))
         if t == 2:
-            gather_third(1, 1)
+            gather_third(1, 0, (1, 3))
+            gather_third(1, 1, (2,))
     gather_last(1, 1)
 
     def late_sums(i, carry):
@@ -358,7 +377,7 @@
         exchange(8 + 2 * t + j, gasend.at[t, j], garecv.at[t, j])
 
     lax.fori_loop(0, 4, proj_own, 0)
-    gather_third(1, 0)
+    gather_third(1, 0, (2,))
     gather_last(1, 0)
     statistics(0)
     attn_exchange(2)
@@ -603,7 +622,7 @@
     scratch = [
         vm((1, 1536), F32), vm((512, 1536), BF16), vm((512, 768), BF16), vm((512, 768), BF16), vm((512, 1536), BF16),
         vm((2, 24, 1536), BF16), vm((2, 24, 1536), F32), vm((24, 128), F32),
-        vm((24, 128), F32), vm((7, 24, 128), F32), vm((2, 3, 24, 768), BF16), vm((2, 2, 48, 768), F32),
+        vm((8, 128), F32), vm((7, 8, 128), F32), vm((2, 3, 24, 768), BF16), vm((2, 2, 48, 768), F32),
         vm((2, 2, 4, 4, 48, 1536), BF16),
         vm((4, 128, 768), BF16), vm((4, 128, 768), BF16), vm((512, 768), F32), vm((512, 768), BF16),
         vm((6, 512, 512), F32), vm((512, 1536), BF16), vm((512, 1536), F32), vm((512, 1536), BF16),

time: 126 us -> 125 us (level)
  no operation moved by 1% of the time
where the time goes in v5:
time: 125 us
  Pallas kernels  124 us (99%)
    pallas_call x1, Pallas kernels, shards(): pl.pallas_call(kernel, out_shape=shapes, in_specs=[hbm] * 5 + [pl.BlockSp...  120 us
    pallas_call x1, Pallas kernels, shards(): pl.pallas_call(place, out_shape=shapes, in_specs=[hbm] * 6, out_specs=[hb...  3.77 us

profile of v5, /device:TPU:1, one launch (start us, length us, event | category | flops | bytes accessed | tf_op | source)
XLA Modules:
  0.0 124.7 jit_solution(1321875725263357120)
XLA Ops:
  0.6 120.1 %sublayer.1 = (bf16[512,1536]{1,0:T(8,128)(2,1)}, bf16[512,1536]{1,0:T(8,128)(2,1)}, bf16[512,768]{1,0:T(8,128)(2,1)}, bf16[512,768]{1,0:T(8,128)(2,1)}, f32[24,1536]{1,0:T(8,128)}, /*index=5*/f32[24,1536]{1,0:T(8,128)}) custom-call(bf16[512,1536]{1,0:T(8,128)(2,1)} %hid_h.1, bf16[512,768]{1,0:T(8,128)(2,1)} %q_h.1, bf16[512,768]{1,0:T(8,128)(2,1)} %k_h.1, ...), custom_call_target="tpu_custom_call" | custom-call | tf_op jit(solution)/shard_map/sublayer/pallas_call | solution.py:647
  120.7 3.8 %place.1 = (bf16[512,1536]{1,0:T(8,128)(2,1)}, bf16[512,1536]{1,0:T(8,128)(2,1)}, bf16[512,768]{1,0:T(8,128)(2,1)}, bf16[512,768]{1,0:T(8,128)(2,1)}, f32[24,1536]{1,0:T(8,128)}, /*index=5*/f32[24,1536]{1,0:T(8,128)}) custom-call(bf16[512,1536]{1,0:T(8,128)(2,1)} %get-tuple-element.12.refs_0_, bf16[512,1536]{1,0:T(8,128)(2,1)} %get-tuple-element.13.refs_1_, ...), custom_call_target="tpu_custom_call" | custom-call | tf_op jit(solution)/shard_map/place/pallas_call | solution.py:658

commit v6 on v5

--- a/solution.py
+++ b/solution.py
@@ -584,13 +584,13 @@
     rs_third(1, 1)
     owner_first(1)
     rs_third(0, 0)
+    rs_third(0, 1)
+    owner_first(0)
     lax.fori_loop(5, 6, bwd, 0)
     outs.append(pltpu.make_async_copy(gq, gq_h, out_m.at[1]))
     outs.append(pltpu.make_async_copy(gk, gk_h, out_m.at[2]))
     outs[-2].start()
     outs[-1].start()
-    rs_third(0, 1)
-    owner_first(0)
     owner_last(1, gwo_h, out_m.at[4])
     owner_last(0, gwv_h, out_m.at[5])
     for w in range(2):

time: 125 us -> 125 us (level)
  no operation moved by 1% of the time
where the time goes in v6:
time: 125 us
  Pallas kernels  124 us (99%)
    pallas_call x1, Pallas kernels, shards(): pl.pallas_call(kernel, out_shape=shapes, in_specs=[hbm] * 5 + [pl.BlockSp...  120 us
    pallas_call x1, Pallas kernels, shards(): pl.pallas_call(place, out_shape=shapes, in_specs=[hbm] * 6, out_specs=[hb...  3.77 us

profile of v6, /device:TPU:1, one launch (start us, length us, event | category | flops | bytes accessed | tf_op | source)
XLA Modules:
  0.0 124.7 jit_solution(15263877975395153588)
XLA Ops:
  0.6 120.1 %sublayer.1 = (bf16[512,1536]{1,0:T(8,128)(2,1)}, bf16[512,1536]{1,0:T(8,128)(2,1)}, bf16[512,768]{1,0:T(8,128)(2,1)}, bf16[512,768]{1,0:T(8,128)(2,1)}, f32[24,1536]{1,0:T(8,128)}, /*index=5*/f32[24,1536]{1,0:T(8,128)}) custom-call(bf16[512,1536]{1,0:T(8,128)(2,1)} %hid_h.1, bf16[512,768]{1,0:T(8,128)(2,1)} %q_h.1, bf16[512,768]{1,0:T(8,128)(2,1)} %k_h.1, ...), custom_call_target="tpu_custom_call" | custom-call | tf_op jit(solution)/shard_map/sublayer/pallas_call | solution.py:647
  120.7 3.8 %place.1 = (bf16[512,1536]{1,0:T(8,128)(2,1)}, bf16[512,1536]{1,0:T(8,128)(2,1)}, bf16[512,768]{1,0:T(8,128)(2,1)}, bf16[512,768]{1,0:T(8,128)(2,1)}, f32[24,1536]{1,0:T(8,128)}, /*index=5*/f32[24,1536]{1,0:T(8,128)}) custom-call(bf16[512,1536]{1,0:T(8,128)(2,1)} %get-tuple-element.12.refs_0_, bf16[512,1536]{1,0:T(8,128)(2,1)} %get-tuple-element.13.refs_1_, ...), custom_call_target="tpu_custom_call" | custom-call | tf_op jit(solution)/shard_map/place/pallas_call | solution.py:658
